TPU v7x, 256 devices: a whole 4x4x8 slice. The times are simulated.
256 devices in a mesh: mem: 8 (over z), space: 32 (over x, y, core).
Axes of the slice: x: 4, y: 4, z: 8, core: 2. Of those that a mesh axis runs over, the one named last changes fastest.
Arguments:
- ensemble: float32 [256, 64, 2048], P('mem', 'space'), may hold values from -6 to 6
- forcing: float32 [64, 2048], P('space'), may hold values from 2 to 8
- obs_cell: int32 [4096], P('space'), may hold values from 0 to 131071, as said below
- obs_value: float32 [4096], P('space'), may hold values from -8 to 8
- obs_var: float32 [4096], P('space'), may hold values from 0.5 to 2
- obs_noise: float32 [256, 4096], P('mem', 'space'), may hold values from -5 to 5
Outputs:
- analysis: float32 [256, 64, 2048], P('mem', 'space')
Inputs may be any that keep to these rules, and one draw needn't show every extreme that they name: `obs_cell`: entries 128 * s to 128 * (s + 1) - 1 name cells of planes 2 * s to 2 * (s + 1) - 1, a cell of plane x and position p having index x * 2048 + p.
All inputs are finite; a program needn't handle non-finite values.
Results may differ from a plain program's by a relative error of at most 0.00018.
Values sent between devices are 32-bit elements; how exact they have to be, the bound alone decides.
A program may use at most 64 MiB of HBM per device.

v0:
```python
import jax
import jax.numpy as jnp
from jax import lax
from jax.experimental import pallas as pl
from jax.experimental.pallas import tpu as pltpu
from jax.sharding import PartitionSpec as P

FSTEPS = 4
ITERS = 6
LOC = 16
REACH = 8
SLOTS = 2 * REACH + 1
MESH = pl.DeviceIdType.MESH
f32 = jnp.float32
bf16 = jnp.bfloat16

R_OUT, R_FORC, R_BACK, R_OBS, R_RHS, R_BAND, R_BOUND = range(7)
R_DIR = 7
R_RIGHT = 12
R_LEFT = 16
RECVS = 20
S_OUT, S_FORC, S_BACK, S_OBS, S_RHS, S_BAND, S_BOUND = range(7)
S_DIR = 7
S_RIGHT = 12
S_LEFT = 16
SENDS = 20

NT = (((1,), (1,)), ((), ()))


def nn(a, b):
    return jnp.dot(a, b, preferred_element_type=f32)


def nt(a, b):
    return lax.dot_general(a, b, NT, preferred_element_type=f32)


def halves(x):
    high = x.astype(bf16)
    return high, (x - high.astype(f32)).astype(bf16)


def awaited(ref, sem):
    pltpu.make_async_copy(ref, ref, sem).wait()


def kernel(
    space_count, mem_count,
    ens, forc, cell, value, var, noise, plane,
    out,
    r, t, fr, zs, oh, ao, ab, ah, al, e0, ex, bb, ch, cl, dh,
    ssem, rsem, lsem,
):
    me_s = lax.axis_index("space")
    me_m = lax.axis_index("mem")
    members = ao.shape[0]
    mdev = noise.shape[0]
    planes = r.shape[0]
    half = mdev // 2
    odev = cell.shape[1]
    slab = ens.shape[2]

    def chunk_of(index):
        return lax.div(index, 2), lax.rem(index, 2)

    def other(base, step, count):
        return lax.rem(base + step, count)

    barrier = pltpu.get_barrier_semaphore()

    def greet_space(i, c):
        pl.semaphore_signal(barrier, inc=1, device_id={"space": other(me_s, i, space_count)}, device_id_type=MESH)
        return c

    def greet_mem(i, c):
        pl.semaphore_signal(barrier, inc=1, device_id={"mem": other(me_m, i, mem_count)}, device_id_type=MESH)
        return c

    lax.fori_loop(1, space_count, greet_space, 0)
    lax.fori_loop(1, mem_count, greet_mem, 0)

    my_c, my_h = chunk_of(me_s)
    own_out = pltpu.make_async_copy(
        ens.at[:, pl.ds(pl.multiple_of(my_h * half, half), half), pl.ds(pl.multiple_of(my_c * 128, 128), 128)],
        r.at[pl.ds(me_s * 2, 2)], lsem.at[0])
    own_forc = pltpu.make_async_copy(
        forc.at[:, pl.ds(pl.multiple_of(my_c * 128, 128), 128)], fr.at[me_s], lsem.at[1])
    own_out.start()
    own_forc.start()

    pl.semaphore_wait(barrier, space_count + mem_count - 2)

    def send_out(i, c):
        to = other(me_s, i, space_count)
        tc, th = chunk_of(to)
        cells = pl.ds(pl.multiple_of(tc * 128, 128), 128)
        pltpu.make_async_remote_copy(
            src_ref=forc.at[:, cells], dst_ref=fr.at[me_s],
            send_sem=ssem.at[S_FORC], recv_sem=rsem.at[R_FORC],
            device_id={"space": to}, device_id_type=MESH).start()
        pltpu.make_async_remote_copy(
            src_ref=ens.at[:, pl.ds(pl.multiple_of(th * half, half), half), cells],
            dst_ref=r.at[pl.ds(me_s * 2, 2)],
            send_sem=ssem.at[S_OUT], recv_sem=rsem.at[R_OUT],
            device_id={"space": to}, device_id_type=MESH).start()
        return c

    lax.fori_loop(1, space_count, send_out, 0)

    cells_here = cell[...]

    def one_hot(i, c):
        rows = lax.broadcasted_iota(jnp.int32, (256, odev), 0) + i * 256
        oh[pl.ds(pl.multiple_of(i * 256, 256), 256), :] = jnp.where(rows == cells_here, 1.0, 0.0).astype(bf16)
        return c

    lax.fori_loop(0, 2 * slab // 256, one_hot, 0)

    own_out.wait()
    own_forc.wait()
    awaited(r.at[pl.ds(0, planes - 2)], rsem.at[R_OUT])
    awaited(fr.at[pl.ds(0, space_count - 1)], rsem.at[R_FORC])

    def advance(src, dst):
        def group(g, carry):
            two, one, now = carry
            for i in range(8):
                x = g * 8 + i
                ahead = src[lax.rem(x + 1, planes)]
                force = fr[g * 4 + i // 2, pl.ds(i % 2, 1), :]
                dst[x] = now + 0.05 * ((ahead - two) * one - now + force)
                two, one, now = one, now, ahead
            return two, one, now

        lax.fori_loop(0, planes // 8, group, (src[planes - 2], src[planes - 1], src[0]))

    for step in range(FSTEPS // 2):
        advance(r, t)
        advance(t, r)

    mine = pl.ds(pl.multiple_of(me_m * mdev, mdev), mdev)
    my_rows = pl.ds(pl.multiple_of(me_m * mdev + my_h * half, half), half)
    my_cells = pl.ds(pl.multiple_of(my_c * 128, 128), 128)

    def send_back(i, c):
        to = other(me_s, i, space_count)
        pltpu.make_async_remote_copy(
            src_ref=r.at[pl.ds(to * 2, 2)], dst_ref=zs.at[:, my_rows, my_cells],
            send_sem=ssem.at[S_BACK], recv_sem=rsem.at[R_BACK],
            device_id={"space": to}, device_id_type=MESH).start()
        return c

    lax.fori_loop(1, space_count, send_back, 0)
    own_back = pltpu.make_async_copy(r.at[pl.ds(me_s * 2, 2)], zs.at[:, my_rows, my_cells], lsem.at[2])
    own_back.start()
    own_back.wait()
    awaited(r.at[pl.ds(0, planes - 2)], rsem.at[R_BACK])

    observed = jnp.zeros((3 * mdev, odev), f32)
    for x in range(2):
        block = zs[x, mine, :]
        first = block.astype(bf16)
        rest = block - first.astype(f32)
        second = rest.astype(bf16)
        third = (rest - second.astype(f32)).astype(bf16)
        pieces = jnp.concatenate([first, second, third], axis=0)
        observed = observed + nn(pieces, oh[x * slab:(x + 1) * slab, :])
    observed = observed[:mdev] + observed[mdev:2 * mdev] + observed[2 * mdev:]
    ao[mine, :] = observed

    def send_obs(i, c):
        pltpu.make_async_remote_copy(
            src_ref=ao.at[mine], dst_ref=ao.at[mine],
            send_sem=ssem.at[S_OBS], recv_sem=rsem.at[R_OBS],
            device_id={"mem": other(me_m, i, mem_count)}, device_id_type=MESH).start()
        return c

    lax.fori_loop(1, mem_count, send_obs, 0)

    plane_row = plane[...]
    rhs = jnp.sqrt(var[...]) * noise[...] + value[...] - observed
    e0[REACH, :mdev, :] = rhs
    e0[REACH, mdev:, :] = jnp.broadcast_to(plane_row, (8, odev))

    def band_send(src, dst_of, send, recv):
        def one(i, c):
            away = (REACH - lax.div(i, 2)) * (1 - 2 * lax.rem(i, 2))
            to = lax.rem(me_s + away + space_count, space_count)
            pltpu.make_async_remote_copy(
                src_ref=src, dst_ref=dst_of(REACH - away),
                send_sem=ssem.at[send], recv_sem=rsem.at[recv],
                device_id={"space": to}, device_id_type=MESH).start()
            return c

        lax.fori_loop(0, 2 * REACH, one, 0)

    band_send(e0.at[REACH], lambda j: e0.at[j], S_RHS, R_RHS)

    awaited(ao.at[pl.ds(0, members - mdev)], rsem.at[R_OBS])
    all_obs = ao[...]
    anom = all_obs - jnp.sum(all_obs, axis=0, keepdims=True) / members
    centre = pl.ds(REACH * odev, odev)
    ab[:, centre] = anom
    band_send(ab.at[:, centre], lambda j: ab.at[:, pl.ds(pl.multiple_of(j * odev, odev), odev)], S_BAND, R_BAND)

    right = other(me_m, 1, mem_count)
    left = other(me_m, mem_count - 1, mem_count)

    def relay(step, way, only=None):
        origin = lax.rem(me_m + mem_count - (step if way > 0 else -step), mem_count)
        rows = pl.ds(pl.multiple_of(origin * mdev, mdev), mdev)
        which = slice(None) if only is None else pl.ds(only, 1)
        ref = zs.at[which, rows, :]
        return pltpu.make_async_remote_copy(
            src_ref=ref, dst_ref=ref,
            send_sem=ssem.at[(S_RIGHT if way > 0 else S_LEFT) + step],
            recv_sem=rsem.at[(R_RIGHT if way > 0 else R_LEFT) + step],
            device_id={"mem": right if way > 0 else left}, device_id_type=MESH)

    def relay_wait(step, only=None):
        for base in (R_RIGHT, R_LEFT):
            if only is None:
                awaited(zs.at[:, pl.ds(0, mdev), :], rsem.at[base + step])
            else:
                awaited(zs.at[pl.ds(0, 1), pl.ds(0, mdev), :], rsem.at[base + step])

    relay(0, 1).start()
    relay(0, -1).start()

    anom_t = anom.T
    th, tl = halves(anom_t)
    both_t = jnp.concatenate([th, tl], axis=0)
    own_plane = jnp.broadcast_to(plane_row, (odev, odev)).T
    own_var = jnp.broadcast_to(var[...], (odev, odev)).T
    diagonal = (lax.broadcasted_iota(jnp.int32, (odev, odev), 0) == lax.broadcasted_iota(jnp.int32, (odev, odev), 1))
    diag_var = jnp.where(diagonal, own_var, 0.0)

    def taper(a, b):
        spread = jnp.abs(a - b)
        spread = jnp.minimum(spread, planes - spread)
        return jnp.maximum(0.0, 1.0 - spread / LOC)

    awaited(e0.at[pl.ds(0, 2 * REACH)], rsem.at[R_RHS])
    awaited(ab.at[:, pl.ds(0, 2 * REACH * odev)], rsem.at[R_BAND])
    relay_wait(0)
    relay(1, 1).start()
    relay(1, -1).start()

    def rows_of(j, total):
        lanes = pl.ds(pl.multiple_of(j * odev, odev), odev)
        high, low = halves(ab[:, lanes])
        ah[:, lanes] = high
        al[:, lanes] = low
        gram = nn(both_t, high)
        gram = gram[:odev] + gram[odev:] + nn(th, low)
        shape = taper(own_plane, e0[j, pl.ds(mdev, 1), :])
        block = shape * gram / (members - 1)
        block = block + jnp.where(j == REACH, 1.0, 0.0) * diag_var
        chigh, clow = halves(block)
        ch[:, lanes] = chigh
        cl[:, lanes] = clow
        dhigh, dlow = halves(e0[j, pl.ds(0, mdev), :])
        dh[:mdev, lanes] = dhigh
        dh[mdev:, lanes] = dlow
        return total + jnp.abs(block)

    total = lax.fori_loop(0, SLOTS, rows_of, jnp.zeros((odev, odev), f32))

    def image_of():
        top = nt(dh[...], ch[...])
        return top[:mdev] + top[mdev:] + nt(dh[:mdev, :], cl[...])

    def load(e):
        def one(j, c):
            lanes = pl.ds(pl.multiple_of(j * odev, odev), odev)
            dhigh, dlow = halves(ex[e, j])
            dh[:mdev, lanes] = dhigh
            dh[mdev:, lanes] = dlow
            return c

        lax.fori_loop(0, SLOTS, one, 0)

    def exchange(e, block):
        ex[e, REACH] = block
        band_send(ex.at[e, REACH], lambda j: ex.at[e, j], S_DIR + e, R_DIR + e)

    def arrived(e):
        awaited(ex.at[e, pl.ds(0, 2 * REACH)], rsem.at[R_DIR + e])

    first_image = image_of()
    exchange(0, first_image)

    row_max = jnp.max(jnp.sum(total, axis=1, keepdims=True), axis=0, keepdims=True)
    var_min = jnp.min(var[...], axis=1, keepdims=True)
    is_upper = lax.broadcasted_iota(jnp.int32, (8, odev), 0) < 4
    bb[me_s] = jnp.where(is_upper, row_max, -var_min)

    def send_bound(i, c):
        pltpu.make_async_remote_copy(
            src_ref=bb.at[me_s], dst_ref=bb.at[me_s],
            send_sem=ssem.at[S_BOUND], recv_sem=rsem.at[R_BOUND],
            device_id={"space": other(me_s, i, space_count)}, device_id_type=MESH).start()
        return c

    lax.fori_loop(1, space_count, send_bound, 0)

    arrived(0)
    load(0)
    second_image = image_of()

    awaited(bb.at[pl.ds(0, space_count - 1)], rsem.at[R_BOUND])
    bounds = jnp.max(bb[...], axis=0)
    upper = bounds[0:1, :]
    lower = -bounds[4:5, :]
    center = (upper + lower) / 2.0
    radius = (upper - lower) / 2.0
    sigma = center / radius
    rho = 1.0 / sigma
    direction = rhs / center
    weight = direction
    residual = rhs - first_image / center
    rho_next = 1.0 / (2.0 * sigma - rho)
    keep, take = rho_next * rho, 2.0 * rho_next / radius
    image = keep * (first_image / center) + take * (first_image - second_image / center)
    direction = keep * direction + take * residual
    rho = rho_next
    weight = weight + direction

    for e in range(1, ITERS - 2):
        residual = residual - image
        rho_next = 1.0 / (2.0 * sigma - rho)
        direction = rho_next * rho * direction + 2.0 * rho_next / radius * residual
        rho = rho_next
        weight = weight + direction
        exchange(e, direction)
        if e == 1:
            relay_wait(1)
            relay(2, 1).start()
            relay(2, -1).start()
        if e == 3:
            relay_wait(2)
            relay(3, 1, 0).start()
            relay(3, -1, 1).start()
        arrived(e)
        load(e)
        image = image_of()
    residual = residual - image
    rho_next = 1.0 / (2.0 * sigma - rho)
    direction = rho_next * rho * direction + 2.0 * rho_next / radius * residual
    weight = weight + direction
    last = ITERS - 2
    exchange(last, weight)
    arrived(last)

    gain = jnp.zeros((2 * mdev, members), f32)
    base = me_s.astype(f32) * 2.0

    def gains(j, total):
        lanes = pl.ds(pl.multiple_of(j * odev, odev), odev)
        row = e0[j, pl.ds(mdev, 1), :]
        block = ex[last, j]
        wide = jnp.concatenate([block * taper(base, row), block * taper(base + 1.0, row)], axis=0)
        high, low = halves(wide)
        top = nt(jnp.concatenate([high, low], axis=0), ah[:, lanes])
        return total + top[:2 * mdev] + top[2 * mdev:] + nt(high, al[:, lanes])

    gain = lax.fori_loop(0, SLOTS, gains, gain) / (members - 1)

    relay_wait(3, 0)

    width = 512
    for x in range(2):
        ghigh, glow = halves(gain[x * mdev:(x + 1) * mdev])
        gboth = jnp.concatenate([ghigh, glow], axis=0)

        def update(i, c, x=x, ghigh=ghigh, gboth=gboth):
            lanes = pl.ds(pl.multiple_of(i * width, width), width)
            states = zs[x, :, lanes]
            states = states - jnp.sum(states, axis=0, keepdims=True) / members
            high, low = halves(states)
            top = nn(gboth, high)
            out[x, :, lanes] = zs[x, mine, lanes] + (top[:mdev] + top[mdev:] + nn(ghigh, low))
            return c

        lax.fori_loop(0, slab // width, update, 0)

    awaited(r.at[pl.ds(0, planes - 2)], ssem.at[S_OUT])
    awaited(fr.at[pl.ds(0, space_count - 1)], ssem.at[S_FORC])
    awaited(r.at[pl.ds(0, planes - 2)], ssem.at[S_BACK])
    awaited(ao.at[pl.ds(0, members - mdev)], ssem.at[S_OBS])
    awaited(e0.at[pl.ds(0, 2 * REACH)], ssem.at[S_RHS])
    awaited(ab.at[:, pl.ds(0, 2 * REACH * odev)], ssem.at[S_BAND])
    awaited(bb.at[pl.ds(0, space_count - 1)], ssem.at[S_BOUND])
    for e in range(ITERS - 1):
        awaited(ex.at[e, pl.ds(0, 2 * REACH)], ssem.at[S_DIR + e])
    for step in range(3):
        for at in (S_RIGHT, S_LEFT):
            awaited(zs.at[:, pl.ds(0, mdev), :], ssem.at[at + step])
    for at in (S_RIGHT, S_LEFT):
        awaited(zs.at[pl.ds(0, 1), pl.ds(0, mdev), :], ssem.at[at + 3])


def shards(ensemble, forcing, obs_cell, obs_value, obs_var, obs_noise):
    mdev, pdev, slab = ensemble.shape
    odev = obs_cell.shape[0]
    space_count = lax.axis_size("space")
    mem_count = lax.axis_size("mem")
    members = mdev * mem_count
    planes = pdev * space_count
    cell = obs_cell - lax.axis_index("space") * (pdev * slab)
    plane = (obs_cell // slab).astype(f32)
    band = SLOTS * odev

    def call(*args):
        return kernel(space_count, mem_count, *args)

    vmem = pl.BlockSpec(memory_space=pltpu.VMEM)
    analysis = pl.pallas_call(
        call,
        out_shape=jax.ShapeDtypeStruct((pdev, mdev, slab), f32),
        in_specs=[vmem] * 7,
        out_specs=vmem,
        scratch_shapes=[
            pltpu.VMEM((planes, mdev // 2, 128), f32),
            pltpu.VMEM((planes, mdev // 2, 128), f32),
            pltpu.VMEM((space_count, pdev, 128), f32),
            pltpu.VMEM((pdev, members, slab), f32),
            pltpu.VMEM((pdev * slab, odev), bf16),
            pltpu.VMEM((members, odev), f32),
            pltpu.VMEM((members, band), f32),
            pltpu.VMEM((members, band), bf16),
            pltpu.VMEM((members, band), bf16),
            pltpu.VMEM((SLOTS, mdev + 8, odev), f32),
            pltpu.VMEM((ITERS - 1, SLOTS, mdev, odev), f32),
            pltpu.VMEM((space_count, 8, odev), f32),
            pltpu.VMEM((odev, band), bf16),
            pltpu.VMEM((odev, band), bf16),
            pltpu.VMEM((2 * mdev, band), bf16),
            pltpu.SemaphoreType.DMA((SENDS,)),
            pltpu.SemaphoreType.DMA((RECVS,)),
            pltpu.SemaphoreType.DMA((3,)),
        ],
        compiler_params=pltpu.CompilerParams(collective_id=0, has_side_effects=True),
        name="cycle",
    )(
        jnp.transpose(ensemble, (1, 0, 2)), forcing, cell[None, :], obs_value[None, :], obs_var[None, :],
        obs_noise, plane[None, :],
    )
    return jnp.transpose(analysis, (1, 0, 2))


def solution(mesh):
    placed = (
        P("mem", "space", None),
        P("space", None),
        P("space"),
        P("space"),
        P("space"),
        P("mem", "space"),
    )
    return jax.shard_map(
        shards, mesh=mesh, in_specs=placed, out_specs=P("mem", "space", None), check_vma=False
    )
```

profile of v0, /device:TPU:1, one launch (start us, length us, event | category | flops | bytes accessed | tf_op | source)
XLA Modules:
  0.0 113.1 jit_solution(14630663079586057002)
XLA Ops:
  0.0 0.0 copy-start
  0.0 0.7 copy-done
  0.7 0.6 convert_bitcast_fusion
  1.2 2.1 %copy.10 = f32[32,2,2048]{2,0,1:T(8,128)} copy(f32[32,2,2048]{2,1,0:T(2,128)} %param.6) | data formatting | bytes 1048576 | tf_op args[0]
  3.4 107.5 %cycle.1 = f32[2,32,2048]{2,1,0:T(8,128)} custom-call(f32[2,32,2048]{2,1,0:T(8,128)} %bitcast.11, f32[2,2048]{1,0:T(2,128)} %args_1_.4, s32[1,128]{1,0:T(1,128)} %get-tuple-element.6.args_2_, f32[1,128]{1,0:T(1,128)} %bitcast.12, f32[1,128]{1,0:T(1,128)} %bitcast.13, f32[32,128]{1,0:T(8,128)} %args_5_.4, f32[1,128]{1,0:T(1,128)} %get-tuple-element.5.args_6_), custom_call_target="tpu_custom_call" | custom-call | tf_op jit(solution)/shard_map/cycle/pallas_call | solution.py:419
  110.9 2.2 %copy.8 = f32[32,2,2048]{2,1,0:T(2,128)} copy(f32[32,2,2048]{2,0,1:T(8,128)} %bitcast.10) | data formatting | bytes 1048576 | tf_op jit(solution)/shard_map/transpose | solution.py:450
Async XLA Ops:
  0.0 0.7 copy-start
where the time goes:
time: 113 us
  Pallas kernels  108 us (96%)
  local copies, waits for them, and re-layouts  5.04 us (4%)
    pallas_call x1, Pallas kernels, shards(): pl.pallas_call(call, out_shape=jax.ShapeDtypeStruct((pdev, mdev, slab), f...  108 us
    unnamed x3, local copies, waits for them, and re-layouts  2.8 us

commit v1 on v0

--- a/solution.py
+++ b/solution.py
@@ -14,16 +14,19 @@
 f32 = jnp.float32
 bf16 = jnp.bfloat16
 
-R_OUT, R_FORC, R_BACK, R_OBS, R_RHS, R_BAND, R_BOUND = range(7)
-R_DIR = 7
-R_RIGHT = 12
-R_LEFT = 16
-RECVS = 20
-S_OUT, S_FORC, S_BACK, S_OBS, S_RHS, S_BAND, S_BOUND = range(7)
-S_DIR = 7
-S_RIGHT = 12
-S_LEFT = 16
-SENDS = 20
+R_OUT, R_FORC, R_BACK, R_RHS, R_BOUND = range(5)
+R_DIR = 5
+R_OBS = 10
+R_BAND = 18
+R_RIGHT = 35
+R_LEFT = 42
+RECVS = 49
+S_OUT, S_FORC, S_BACK, S_OBS, S_RHS, S_BAND, S_PAIR, S_BOUND = range(8)
+S_DIR = 8
+S_RIGHT = 13
+S_LEFT = 20
+SENDS = 27
+HOPS = 7
 
 NT = (((1,), (1,)), ((), ()))
 
@@ -49,12 +52,12 @@
     space_count, mem_count,
     ens, forc, cell, value, var, noise, plane,
     out,
-    r, t, fr, zs, oh, ao, ab, ah, al, e0, ex, bb, ch, cl, dh,
+    r, t, fr, zs, sh, sl, oh, ab, ah, al, e0, ex, bb, ch, cl, dh, gh,
     ssem, rsem, lsem,
 ):
     me_s = lax.axis_index("space")
     me_m = lax.axis_index("mem")
-    members = ao.shape[0]
+    members = ab.shape[1]
     mdev = noise.shape[0]
     planes = r.shape[0]
     half = mdev // 2
@@ -167,25 +170,48 @@
         pieces = jnp.concatenate([first, second, third], axis=0)
         observed = observed + nn(pieces, oh[x * slab:(x + 1) * slab, :])
     observed = observed[:mdev] + observed[mdev:2 * mdev] + observed[2 * mdev:]
-    ao[mine, :] = observed
+    ab[REACH, mine, :] = observed
 
     def send_obs(i, c):
         pltpu.make_async_remote_copy(
-            src_ref=ao.at[mine], dst_ref=ao.at[mine],
-            send_sem=ssem.at[S_OBS], recv_sem=rsem.at[R_OBS],
+            src_ref=ab.at[REACH, mine], dst_ref=ab.at[REACH, mine],
+            send_sem=ssem.at[S_OBS], recv_sem=rsem.at[R_OBS + i],
             device_id={"mem": other(me_m, i, mem_count)}, device_id_type=MESH).start()
         return c
 
     lax.fori_loop(1, mem_count, send_obs, 0)
+
+    right = other(me_m, 1, mem_count)
+    left = other(me_m, mem_count - 1, mem_count)
+
+    def relay(hop):
+        for way in (1, -1):
+            origin = lax.rem(me_m + mem_count - way * (hop // 2), mem_count)
+            x = hop % 2 if way > 0 else 1 - hop % 2
+            ref = zs.at[x, pl.ds(pl.multiple_of(origin * mdev, mdev), mdev), :]
+            pltpu.make_async_remote_copy(
+                src_ref=ref, dst_ref=ref,
+                send_sem=ssem.at[(S_RIGHT if way > 0 else S_LEFT) + hop],
+                recv_sem=rsem.at[(R_RIGHT if way > 0 else R_LEFT) + hop],
+                device_id={"mem": right if way > 0 else left}, device_id_type=MESH).start()
+
+    def relayed(hop):
+        for base in (R_RIGHT, R_LEFT):
+            awaited(zs.at[0, pl.ds(0, mdev), :], rsem.at[base + hop])
 
     plane_row = plane[...]
     rhs = jnp.sqrt(var[...]) * noise[...] + value[...] - observed
     e0[REACH, :mdev, :] = rhs
     e0[REACH, mdev:, :] = jnp.broadcast_to(plane_row, (8, odev))
 
+    def spread_of(n, unit):
+        at = lax.div(n, 2)
+        far = lax.div(at + 1, 2) * (1 - 2 * lax.rem(at + 1, 2))
+        return (REACH // (2 * unit) + far) * unit * (1 - 2 * lax.rem(n, 2))
+
     def band_send(src, dst_of, send, recv):
         def one(i, c):
-            away = (REACH - lax.div(i, 2)) * (1 - 2 * lax.rem(i, 2))
+            away = spread_of(i, 1)
             to = lax.rem(me_s + away + space_count, space_count)
             pltpu.make_async_remote_copy(
                 src_ref=src, dst_ref=dst_of(REACH - away),
@@ -197,38 +223,63 @@
 
     band_send(e0.at[REACH], lambda j: e0.at[j], S_RHS, R_RHS)
 
-    awaited(ao.at[pl.ds(0, members - mdev)], rsem.at[R_OBS])
-    all_obs = ao[...]
-    anom = all_obs - jnp.sum(all_obs, axis=0, keepdims=True) / members
-    centre = pl.ds(REACH * odev, odev)
-    ab[:, centre] = anom
-    band_send(ab.at[:, centre], lambda j: ab.at[:, pl.ds(pl.multiple_of(j * odev, odev), odev)], S_BAND, R_BAND)
-
-    right = other(me_m, 1, mem_count)
-    left = other(me_m, mem_count - 1, mem_count)
-
-    def relay(step, way, only=None):
-        origin = lax.rem(me_m + mem_count - (step if way > 0 else -step), mem_count)
+    def piece_to(step, i):
+        away = spread_of(i, 2)
+        origin = lax.rem(me_m + mem_count - step, mem_count)
         rows = pl.ds(pl.multiple_of(origin * mdev, mdev), mdev)
-        which = slice(None) if only is None else pl.ds(only, 1)
-        ref = zs.at[which, rows, :]
-        return pltpu.make_async_remote_copy(
-            src_ref=ref, dst_ref=ref,
-            send_sem=ssem.at[(S_RIGHT if way > 0 else S_LEFT) + step],
-            recv_sem=rsem.at[(R_RIGHT if way > 0 else R_LEFT) + step],
-            device_id={"mem": right if way > 0 else left}, device_id_type=MESH)
-
-    def relay_wait(step, only=None):
-        for base in (R_RIGHT, R_LEFT):
-            if only is None:
-                awaited(zs.at[:, pl.ds(0, mdev), :], rsem.at[base + step])
-            else:
-                awaited(zs.at[pl.ds(0, 1), pl.ds(0, mdev), :], rsem.at[base + step])
-
-    relay(0, 1).start()
-    relay(0, -1).start()
-
-    anom_t = anom.T
+        pltpu.make_async_remote_copy(
+            src_ref=ab.at[REACH, rows], dst_ref=ab.at[REACH - away, rows],
+            send_sem=ssem.at[S_BAND], recv_sem=rsem.at[R_BAND + REACH - away],
+            device_id={"space": lax.rem(me_s + away + space_count, space_count)}, device_id_type=MESH).start()
+
+    def piece_here(step):
+        awaited(ab.at[REACH, pl.ds(0, mdev)], rsem.at[R_OBS + step])
+
+    def to_chips(step):
+        def one(i, c):
+            piece_to(step, i)
+            return c
+
+        lax.fori_loop(0, REACH, one, 0)
+
+    to_chips(0)
+    relay(0)
+    relay(1)
+    early = (1, mem_count - 1)
+    for step in early:
+        piece_here(step)
+        to_chips(step)
+    for step in range(2, mem_count - 1):
+        piece_here(step)
+
+    def late(i, c):
+        def one(step, d):
+            piece_to(step, i)
+            return d
+
+        return lax.fori_loop(2, mem_count - 1, one, c)
+
+    lax.fori_loop(0, REACH, late, 0)
+
+    turn = 1 - 2 * my_h
+    partner = me_s + turn
+
+    def pair_send(e):
+        pltpu.make_async_remote_copy(
+            src_ref=ab.at[REACH + turn * e], dst_ref=ab.at[REACH + turn * (e - 1)],
+            send_sem=ssem.at[S_PAIR], recv_sem=rsem.at[R_BAND + REACH + turn * (e - 1)],
+            device_id={"space": partner}, device_id_type=MESH).start()
+
+    def slot_here(j):
+        awaited(ab.at[0], rsem.at[R_BAND + j])
+
+    pair_send(0)
+
+    def anomalies(j):
+        raw = ab[j]
+        return raw - jnp.sum(raw, axis=0, keepdims=True) / members
+
+    anom_t = anomalies(REACH).T
     th, tl = halves(anom_t)
     both_t = jnp.concatenate([th, tl], axis=0)
     own_plane = jnp.broadcast_to(plane_row, (odev, odev)).T
@@ -241,22 +292,16 @@
         spread = jnp.minimum(spread, planes - spread)
         return jnp.maximum(0.0, 1.0 - spread / LOC)
 
-    awaited(e0.at[pl.ds(0, 2 * REACH)], rsem.at[R_RHS])
-    awaited(ab.at[:, pl.ds(0, 2 * REACH * odev)], rsem.at[R_BAND])
-    relay_wait(0)
-    relay(1, 1).start()
-    relay(1, -1).start()
-
-    def rows_of(j, total):
+    def rows_of(j, total, more=None):
         lanes = pl.ds(pl.multiple_of(j * odev, odev), odev)
-        high, low = halves(ab[:, lanes])
+        high, low = halves(anomalies(j))
         ah[:, lanes] = high
         al[:, lanes] = low
         gram = nn(both_t, high)
         gram = gram[:odev] + gram[odev:] + nn(th, low)
-        shape = taper(own_plane, e0[j, pl.ds(mdev, 1), :])
-        block = shape * gram / (members - 1)
-        block = block + jnp.where(j == REACH, 1.0, 0.0) * diag_var
+        block = taper(own_plane, e0[j, pl.ds(mdev, 1), :]) * gram / (members - 1)
+        if more is not None:
+            block = block + more
         chigh, clow = halves(block)
         ch[:, lanes] = chigh
         cl[:, lanes] = clow
@@ -265,7 +310,31 @@
         dh[mdev:, lanes] = dlow
         return total + jnp.abs(block)
 
-    total = lax.fori_loop(0, SLOTS, rows_of, jnp.zeros((odev, odev), f32))
+    total = rows_of(REACH, jnp.zeros((odev, odev), f32), diag_var)
+    awaited(e0.at[pl.ds(0, 2 * REACH)], rsem.at[R_RHS])
+    relayed(0)
+    relay(2)
+
+    def from_partner(e, total):
+        j = REACH + turn * (1 - e)
+        slot_here(j)
+        return rows_of(j, total)
+
+    def two_slots(i, total):
+        e = spread_of(i, 2)
+        j = REACH + turn * e
+        slot_here(j)
+        pair_send(e)
+        total = rows_of(j, total)
+        return from_partner(jnp.where(i == 0, 0, spread_of(lax.max(i - 1, 0), 2)), total)
+
+    total = lax.fori_loop(0, REACH - 1, two_slots, total)
+    final = REACH - turn * REACH
+    slot_here(final)
+    total = rows_of(final, total)
+    total = from_partner(spread_of(REACH - 2, 2), total)
+    relayed(1)
+    relay(3)
 
     def image_of():
         top = nt(dh[...], ch[...])
@@ -306,6 +375,8 @@
     lax.fori_loop(1, space_count, send_bound, 0)
 
     arrived(0)
+    relayed(2)
+    relay(4)
     load(0)
     second_image = image_of()
 
@@ -334,15 +405,10 @@
         rho = rho_next
         weight = weight + direction
         exchange(e, direction)
-        if e == 1:
-            relay_wait(1)
-            relay(2, 1).start()
-            relay(2, -1).start()
-        if e == 3:
-            relay_wait(2)
-            relay(3, 1, 0).start()
-            relay(3, -1, 1).start()
         arrived(e)
+        if e < 3:
+            relayed(e + 2)
+            relay(e + 4)
         load(e)
         image = image_of()
     residual = residual - image
@@ -351,36 +417,47 @@
     weight = weight + direction
     last = ITERS - 2
     exchange(last, weight)
+
+    relayed(HOPS - 2)
+    relayed(HOPS - 1)
+    width = 512
+
+    def split_states(i, c):
+        x = lax.div(i, slab // width)
+        lanes = pl.ds(pl.multiple_of(lax.rem(i, slab // width) * width, width), width)
+        states = zs[x, :, lanes]
+        high, low = halves(states - jnp.sum(states, axis=0, keepdims=True) / members)
+        sh[x, :, lanes] = high
+        sl[x, :, lanes] = low
+        return c
+
+    lax.fori_loop(0, 2 * slab // width, split_states, 0)
     arrived(last)
 
-    gain = jnp.zeros((2 * mdev, members), f32)
     base = me_s.astype(f32) * 2.0
 
-    def gains(j, total):
+    def tapered(j, c):
         lanes = pl.ds(pl.multiple_of(j * odev, odev), odev)
         row = e0[j, pl.ds(mdev, 1), :]
         block = ex[last, j]
-        wide = jnp.concatenate([block * taper(base, row), block * taper(base + 1.0, row)], axis=0)
-        high, low = halves(wide)
-        top = nt(jnp.concatenate([high, low], axis=0), ah[:, lanes])
-        return total + top[:2 * mdev] + top[2 * mdev:] + nt(high, al[:, lanes])
-
-    gain = lax.fori_loop(0, SLOTS, gains, gain) / (members - 1)
-
-    relay_wait(3, 0)
-
-    width = 512
+        for x in range(2):
+            high, low = halves(block * taper(base + x, row))
+            gh[x * mdev:(x + 1) * mdev, lanes] = high
+            gh[(2 + x) * mdev:(3 + x) * mdev, lanes] = low
+        return c
+
+    lax.fori_loop(0, SLOTS, tapered, 0)
+    top = nt(gh[...], ah[...])
+    gain = (top[:2 * mdev] + top[2 * mdev:] + nt(gh[:2 * mdev, :], al[...])) / (members - 1)
+
     for x in range(2):
         ghigh, glow = halves(gain[x * mdev:(x + 1) * mdev])
         gboth = jnp.concatenate([ghigh, glow], axis=0)
 
         def update(i, c, x=x, ghigh=ghigh, gboth=gboth):
             lanes = pl.ds(pl.multiple_of(i * width, width), width)
-            states = zs[x, :, lanes]
-            states = states - jnp.sum(states, axis=0, keepdims=True) / members
-            high, low = halves(states)
-            top = nn(gboth, high)
-            out[x, :, lanes] = zs[x, mine, lanes] + (top[:mdev] + top[mdev:] + nn(ghigh, low))
+            top = nn(gboth, sh[x, :, lanes])
+            out[x, :, lanes] = zs[x, mine, lanes] + (top[:mdev] + top[mdev:] + nn(ghigh, sl[x, :, lanes]))
             return c
 
         lax.fori_loop(0, slab // width, update, 0)
@@ -388,17 +465,16 @@
     awaited(r.at[pl.ds(0, planes - 2)], ssem.at[S_OUT])
     awaited(fr.at[pl.ds(0, space_count - 1)], ssem.at[S_FORC])
     awaited(r.at[pl.ds(0, planes - 2)], ssem.at[S_BACK])
-    awaited(ao.at[pl.ds(0, members - mdev)], ssem.at[S_OBS])
+    awaited(ab.at[0, pl.ds(0, members - mdev)], ssem.at[S_OBS])
     awaited(e0.at[pl.ds(0, 2 * REACH)], ssem.at[S_RHS])
-    awaited(ab.at[:, pl.ds(0, 2 * REACH * odev)], ssem.at[S_BAND])
+    awaited(ab.at[pl.ds(0, REACH)], ssem.at[S_BAND])
+    awaited(ab.at[pl.ds(0, REACH)], ssem.at[S_PAIR])
     awaited(bb.at[pl.ds(0, space_count - 1)], ssem.at[S_BOUND])
     for e in range(ITERS - 1):
         awaited(ex.at[e, pl.ds(0, 2 * REACH)], ssem.at[S_DIR + e])
-    for step in range(3):
+    for hop in range(HOPS):
         for at in (S_RIGHT, S_LEFT):
-            awaited(zs.at[:, pl.ds(0, mdev), :], ssem.at[at + step])
-    for at in (S_RIGHT, S_LEFT):
-        awaited(zs.at[pl.ds(0, 1), pl.ds(0, mdev), :], ssem.at[at + 3])
+            awaited(zs.at[0, pl.ds(0, mdev), :], ssem.at[at + hop])
 
 
 def shards(ensemble, forcing, obs_cell, obs_value, obs_var, obs_noise):
@@ -426,9 +502,10 @@
             pltpu.VMEM((planes, mdev // 2, 128), f32),
             pltpu.VMEM((space_count, pdev, 128), f32),
             pltpu.VMEM((pdev, members, slab), f32),
+            pltpu.VMEM((pdev, members, slab), bf16),
+            pltpu.VMEM((pdev, members, slab), bf16),
             pltpu.VMEM((pdev * slab, odev), bf16),
-            pltpu.VMEM((members, odev), f32),
-            pltpu.VMEM((members, band), f32),
+            pltpu.VMEM((SLOTS, members, odev), f32),
             pltpu.VMEM((members, band), bf16),
             pltpu.VMEM((members, band), bf16),
             pltpu.VMEM((SLOTS, mdev + 8, odev), f32),
@@ -437,6 +514,7 @@
             pltpu.VMEM((odev, band), bf16),
             pltpu.VMEM((odev, band), bf16),
             pltpu.VMEM((2 * mdev, band), bf16),
+            pltpu.VMEM((2 * pdev * mdev, band), bf16),
             pltpu.SemaphoreType.DMA((SENDS,)),
             pltpu.SemaphoreType.DMA((RECVS,)),
             pltpu.SemaphoreType.DMA((3,)),

time: 113 us -> 94.3 us (0.83)
  Pallas kernels: 108 us -> 88.5 us
    pallas_call x1, Pallas kernels: 108 us -> 88.5 us  [shards(): pl.pallas_call(call, out_shape=jax.ShapeDtypeStruct((pdev, mdev, slab), f...]
where the time goes in v1:
time: 94.3 us; the launch traced here: 94.1 us
  Pallas kernels  88.5 us (94%)
  local copies, waits for them, and re-layouts  5.04 us (5%)
    pallas_call x1, Pallas kernels, shards(): pl.pallas_call(call, out_shape=jax.ShapeDtypeStruct((pdev, mdev, slab), f...  88.5 us
    unnamed x3, local copies, waits for them, and re-layouts  2.8 us
    transpose x1, local copies, waits for them, and re-layouts, shards(): return jnp.transpose(analysis, (1, 0, 2))  2.24 us

profile of v1, /device:TPU:1, one launch (start us, length us, event | category | flops | bytes accessed | tf_op | source)
XLA Modules:
  0.0 94.1 jit_solution(13203096872696069475)
XLA Ops:
  0.0 0.0 copy-start
  0.0 0.7 copy-done
  0.7 0.6 convert_bitcast_fusion
  1.2 2.1 %copy.10 = f32[32,2,2048]{2,0,1:T(8,128)} copy(f32[32,2,2048]{2,1,0:T(2,128)} %param.6) | data formatting | bytes 1048576 | tf_op args[0]
  3.4 88.5 %cycle.1 = f32[2,32,2048]{2,1,0:T(8,128)} custom-call(f32[2,32,2048]{2,1,0:T(8,128)} %bitcast.11, f32[2,2048]{1,0:T(2,128)} %args_1_.4, s32[1,128]{1,0:T(1,128)} %get-tuple-element.6.args_2_, f32[1,128]{1,0:T(1,128)} %bitcast.12, f32[1,128]{1,0:T(1,128)} %bitcast.13, f32[32,128]{1,0:T(8,128)} %args_5_.4, f32[1,128]{1,0:T(1,128)} %get-tuple-element.5.args_6_), custom_call_target="tpu_custom_call" | custom-call | tf_op jit(solution)/shard_map/cycle/pallas_call | solution.py:495
  91.9 2.2 %copy.8 = f32[32,2,2048]{2,1,0:T(2,128)} copy(f32[32,2,2048]{2,0,1:T(8,128)} %bitcast.10) | data formatting | bytes 1048576 | tf_op jit(solution)/shard_map/transpose | solution.py:528
Async XLA Ops:
  0.0 0.7 copy-start

commit v2 on v1

--- a/solution.py
+++ b/solution.py
@@ -14,19 +14,21 @@
 f32 = jnp.float32
 bf16 = jnp.bfloat16
 
+GROUP = 4
+GROUPS = 2 * REACH // GROUP
+HOPS = 7
 R_OUT, R_FORC, R_BACK, R_RHS, R_BOUND = range(5)
 R_DIR = 5
-R_OBS = 10
-R_BAND = 18
-R_RIGHT = 35
-R_LEFT = 42
-RECVS = 49
+R_OBS = R_DIR + GROUPS * (ITERS - 1)
+R_BAND = R_OBS + 8
+R_RIGHT = R_BAND + SLOTS
+R_LEFT = R_RIGHT + HOPS
+RECVS = R_LEFT + HOPS
 S_OUT, S_FORC, S_BACK, S_OBS, S_RHS, S_BAND, S_PAIR, S_BOUND = range(8)
 S_DIR = 8
-S_RIGHT = 13
-S_LEFT = 20
-SENDS = 27
-HOPS = 7
+S_RIGHT = S_DIR + ITERS - 1
+S_LEFT = S_RIGHT + HOPS
+SENDS = S_LEFT + HOPS
 
 NT = (((1,), (1,)), ((), ()))
 
@@ -50,9 +52,9 @@
 
 def kernel(
     space_count, mem_count,
-    ens, forc, cell, value, var, noise, plane,
+    ens, forc, cell, value, var, noise,
     out,
-    r, t, fr, zs, sh, sl, oh, ab, ah, al, e0, ex, bb, ch, cl, dh, gh,
+    r, t, fr, zs, sh, sl, oh, ab, ah, al, e0, ex, bb, ch, cl,
     ssem, rsem, lsem,
 ):
     me_s = lax.axis_index("space")
@@ -111,7 +113,7 @@
 
     lax.fori_loop(1, space_count, send_out, 0)
 
-    cells_here = cell[...]
+    cells_here = cell[...] - me_s * (2 * slab)
 
     def one_hot(i, c):
         rows = lax.broadcasted_iota(jnp.int32, (256, odev), 0) + i * 256
@@ -199,38 +201,48 @@
         for base in (R_RIGHT, R_LEFT):
             awaited(zs.at[0, pl.ds(0, mdev), :], rsem.at[base + hop])
 
-    plane_row = plane[...]
+    plane_row = jnp.floor(cell[...].astype(f32) / slab)
     rhs = jnp.sqrt(var[...]) * noise[...] + value[...] - observed
-    e0[REACH, :mdev, :] = rhs
-    e0[REACH, mdev:, :] = jnp.broadcast_to(plane_row, (8, odev))
-
-    def spread_of(n, unit):
+    own = 2 * REACH
+    e0[own, :mdev, :] = rhs
+    e0[own, mdev:, :] = jnp.broadcast_to(plane_row, (8, odev))
+
+    def away_at(n):
         at = lax.div(n, 2)
         far = lax.div(at + 1, 2) * (1 - 2 * lax.rem(at + 1, 2))
-        return (REACH // (2 * unit) + far) * unit * (1 - 2 * lax.rem(n, 2))
-
-    def band_send(src, dst_of, send, recv):
+        return (REACH // 2 + far) * (1 - 2 * lax.rem(n, 2))
+
+    def place_of(away):
+        past = lax.max(away, -away) - REACH // 2
+        rank = 2 * lax.max(past, -past) - jnp.where(past > 0, 1, 0)
+        return 2 * rank + jnp.where(away < 0, 1, 0)
+
+    def band_send(src, dst_of, send, recv_of):
         def one(i, c):
-            away = spread_of(i, 1)
+            away = away_at(i)
             to = lax.rem(me_s + away + space_count, space_count)
+            there = i + 1 - 2 * lax.rem(i, 2)
             pltpu.make_async_remote_copy(
-                src_ref=src, dst_ref=dst_of(REACH - away),
-                send_sem=ssem.at[send], recv_sem=rsem.at[recv],
+                src_ref=src, dst_ref=dst_of(there),
+                send_sem=ssem.at[send], recv_sem=rsem.at[recv_of(there)],
                 device_id={"space": to}, device_id_type=MESH).start()
             return c
 
         lax.fori_loop(0, 2 * REACH, one, 0)
 
-    band_send(e0.at[REACH], lambda j: e0.at[j], S_RHS, R_RHS)
+    band_send(e0.at[own], lambda j: e0.at[j], S_RHS, lambda j: R_RHS)
+
+    def space_at(chips):
+        return {"space": lax.rem(me_s + 2 * chips + space_count, space_count)}
 
     def piece_to(step, i):
-        away = spread_of(i, 2)
+        chips = (1 + 3 * lax.div(i, 2)) * (1 - 2 * lax.rem(i, 2))
         origin = lax.rem(me_m + mem_count - step, mem_count)
         rows = pl.ds(pl.multiple_of(origin * mdev, mdev), mdev)
         pltpu.make_async_remote_copy(
-            src_ref=ab.at[REACH, rows], dst_ref=ab.at[REACH - away, rows],
-            send_sem=ssem.at[S_BAND], recv_sem=rsem.at[R_BAND + REACH - away],
-            device_id={"space": lax.rem(me_s + away + space_count, space_count)}, device_id_type=MESH).start()
+            src_ref=ab.at[REACH, rows], dst_ref=ab.at[REACH - 2 * chips, rows],
+            send_sem=ssem.at[S_BAND], recv_sem=rsem.at[R_BAND + REACH - 2 * chips],
+            device_id=space_at(chips), device_id_type=MESH).start()
 
     def piece_here(step):
         awaited(ab.at[REACH, pl.ds(0, mdev)], rsem.at[R_OBS + step])
@@ -240,26 +252,15 @@
             piece_to(step, i)
             return c
 
-        lax.fori_loop(0, REACH, one, 0)
+        lax.fori_loop(0, 4, one, 0)
 
     to_chips(0)
     relay(0)
     relay(1)
-    early = (1, mem_count - 1)
-    for step in early:
-        piece_here(step)
-        to_chips(step)
-    for step in range(2, mem_count - 1):
-        piece_here(step)
-
-    def late(i, c):
-        def one(step, d):
-            piece_to(step, i)
-            return d
-
-        return lax.fori_loop(2, mem_count - 1, one, c)
-
-    lax.fori_loop(0, REACH, late, 0)
+    for away in range(1, mem_count // 2 + 1):
+        for step in sorted({away, mem_count - away}):
+            piece_here(step)
+            to_chips(step)
 
     turn = 1 - 2 * my_h
     partner = me_s + turn
@@ -292,72 +293,104 @@
         spread = jnp.minimum(spread, planes - spread)
         return jnp.maximum(0.0, 1.0 - spread / LOC)
 
-    def rows_of(j, total, more=None):
-        lanes = pl.ds(pl.multiple_of(j * odev, odev), odev)
+    def rows_of(j, place, total, more=None):
+        lanes = pl.ds(pl.multiple_of(place * odev, odev), odev)
         high, low = halves(anomalies(j))
         ah[:, lanes] = high
         al[:, lanes] = low
         gram = nn(both_t, high)
         gram = gram[:odev] + gram[odev:] + nn(th, low)
-        block = taper(own_plane, e0[j, pl.ds(mdev, 1), :]) * gram / (members - 1)
+        block = taper(own_plane, e0[place, pl.ds(mdev, 1), :]) * gram / (members - 1)
         if more is not None:
             block = block + more
         chigh, clow = halves(block)
         ch[:, lanes] = chigh
         cl[:, lanes] = clow
-        dhigh, dlow = halves(e0[j, pl.ds(0, mdev), :])
-        dh[:mdev, lanes] = dhigh
-        dh[mdev:, lanes] = dlow
         return total + jnp.abs(block)
 
-    total = rows_of(REACH, jnp.zeros((odev, odev), f32), diag_var)
+    total = rows_of(REACH, own, jnp.zeros((odev, odev), f32), diag_var)
+
+    for side in (1, -1):
+        slot = REACH + 2 * side
+        slot_here(slot)
+        for chips in (-side, 4 * side):
+            there = REACH + 2 * (side - chips)
+            pltpu.make_async_remote_copy(
+                src_ref=ab.at[slot], dst_ref=ab.at[there],
+                send_sem=ssem.at[S_BAND], recv_sem=rsem.at[R_BAND + there],
+                device_id=space_at(chips), device_id_type=MESH).start()
+    pair_send(2)
+    pair_send(-2)
     awaited(e0.at[pl.ds(0, 2 * REACH)], rsem.at[R_RHS])
+
+    def slot_rows(e, total):
+        return rows_of(REACH + turn * e, place_of(turn * e), total)
+
+    def from_partner(e, total):
+        slot_here(REACH + turn * (1 - e))
+        return slot_rows(1 - e, total)
+
+    total = slot_rows(2, total)
+    total = slot_rows(-2, total)
+    total = from_partner(0, total)
     relayed(0)
     relay(2)
 
-    def from_partner(e, total):
-        j = REACH + turn * (1 - e)
-        slot_here(j)
-        return rows_of(j, total)
+    def pick(i, table):
+        value = table[0]
+        for k in range(1, len(table)):
+            value = jnp.where(i == k, table[k], value)
+        return value
 
     def two_slots(i, total):
-        e = spread_of(i, 2)
-        j = REACH + turn * e
-        slot_here(j)
+        e = pick(i, (8, 4, -4, 6, -6))
+        slot_here(REACH + turn * e)
         pair_send(e)
-        total = rows_of(j, total)
-        return from_partner(jnp.where(i == 0, 0, spread_of(lax.max(i - 1, 0), 2)), total)
-
-    total = lax.fori_loop(0, REACH - 1, two_slots, total)
-    final = REACH - turn * REACH
-    slot_here(final)
-    total = rows_of(final, total)
-    total = from_partner(spread_of(REACH - 2, 2), total)
+        total = slot_rows(e, total)
+        return from_partner(pick(i, (2, -2, 8, 4, -4)), total)
+
+    total = lax.fori_loop(0, 5, two_slots, total)
+    slot_here(REACH - turn * REACH)
+    total = slot_rows(-REACH, total)
+
+    def last_two(i, total):
+        return from_partner(pick(i, (6, -6)), total)
+
+    total = lax.fori_loop(0, 2, last_two, total)
     relayed(1)
     relay(3)
 
-    def image_of():
-        top = nt(dh[...], ch[...])
-        return top[:mdev] + top[mdev:] + nt(dh[:mdev, :], cl[...])
-
-    def load(e):
-        def one(j, c):
-            lanes = pl.ds(pl.multiple_of(j * odev, odev), odev)
-            dhigh, dlow = halves(ex[e, j])
-            dh[:mdev, lanes] = dhigh
-            dh[mdev:, lanes] = dlow
-            return c
-
-        lax.fori_loop(0, SLOTS, one, 0)
+    def part(block, lanes):
+        high, low = halves(block)
+        top = nt(jnp.concatenate([high, low], axis=0), ch[:, lanes])
+        return top[:mdev] + top[mdev:] + nt(high, cl[:, lanes])
+
+    def lanes_of(g):
+        return slice(g * GROUP * odev, (g + 1) * GROUP * odev)
+
+    own_lanes = slice(own * odev, (own + 1) * odev)
+
+    def image_of(block, group):
+        image = part(block, own_lanes)
+        for g in range(GROUPS):
+            image = image + part(group(g), lanes_of(g))
+        return image
+
+    def rhs_group(g):
+        return jnp.concatenate([e0[g * GROUP + k, :mdev, :] for k in range(GROUP)], axis=1)
 
     def exchange(e, block):
-        ex[e, REACH] = block
-        band_send(ex.at[e, REACH], lambda j: ex.at[e, j], S_DIR + e, R_DIR + e)
+        ex[e, own] = block
+        band_send(ex.at[e, own], lambda j: ex.at[e, j], S_DIR + e, lambda j: R_DIR + GROUPS * e + lax.div(j, GROUP))
 
     def arrived(e):
-        awaited(ex.at[e, pl.ds(0, 2 * REACH)], rsem.at[R_DIR + e])
-
-    first_image = image_of()
+        def group(g):
+            awaited(ex.at[e, pl.ds(g * GROUP, GROUP)], rsem.at[R_DIR + GROUPS * e + g])
+            return jnp.concatenate([ex[e, g * GROUP + k] for k in range(GROUP)], axis=1)
+
+        return group
+
+    first_image = image_of(rhs, rhs_group)
     exchange(0, first_image)
 
     row_max = jnp.max(jnp.sum(total, axis=1, keepdims=True), axis=0, keepdims=True)
@@ -374,11 +407,9 @@
 
     lax.fori_loop(1, space_count, send_bound, 0)
 
-    arrived(0)
+    second_image = image_of(first_image, arrived(0))
     relayed(2)
     relay(4)
-    load(0)
-    second_image = image_of()
 
     awaited(bb.at[pl.ds(0, space_count - 1)], rsem.at[R_BOUND])
     bounds = jnp.max(bb[...], axis=0)
@@ -405,12 +436,10 @@
         rho = rho_next
         weight = weight + direction
         exchange(e, direction)
-        arrived(e)
+        image = image_of(direction, arrived(e))
         if e < 3:
             relayed(e + 2)
             relay(e + 4)
-        load(e)
-        image = image_of()
     residual = residual - image
     rho_next = 1.0 / (2.0 * sigma - rho)
     direction = rho_next * rho * direction + 2.0 * rho_next / radius * residual
@@ -432,23 +461,21 @@
         return c
 
     lax.fori_loop(0, 2 * slab // width, split_states, 0)
-    arrived(last)
 
     base = me_s.astype(f32) * 2.0
 
-    def tapered(j, c):
-        lanes = pl.ds(pl.multiple_of(j * odev, odev), odev)
-        row = e0[j, pl.ds(mdev, 1), :]
-        block = ex[last, j]
-        for x in range(2):
-            high, low = halves(block * taper(base + x, row))
-            gh[x * mdev:(x + 1) * mdev, lanes] = high
-            gh[(2 + x) * mdev:(3 + x) * mdev, lanes] = low
-        return c
-
-    lax.fori_loop(0, SLOTS, tapered, 0)
-    top = nt(gh[...], ah[...])
-    gain = (top[:2 * mdev] + top[2 * mdev:] + nt(gh[:2 * mdev, :], al[...])) / (members - 1)
+    def gain_part(block, row, lanes):
+        wide = jnp.concatenate([block * taper(base, row), block * taper(base + 1.0, row)], axis=0)
+        high, low = halves(wide)
+        top = nt(jnp.concatenate([high, low], axis=0), ah[:, lanes])
+        return top[:2 * mdev] + top[2 * mdev:] + nt(high, al[:, lanes])
+
+    gain = gain_part(weight, plane_row, own_lanes)
+    group = arrived(last)
+    for g in range(GROUPS):
+        rows = jnp.concatenate([e0[g * GROUP + k, pl.ds(mdev, 1), :] for k in range(GROUP)], axis=1)
+        gain = gain + gain_part(group(g), rows, lanes_of(g))
+    gain = gain / (members - 1)
 
     for x in range(2):
         ghigh, glow = halves(gain[x * mdev:(x + 1) * mdev])
@@ -484,8 +511,6 @@
     mem_count = lax.axis_size("mem")
     members = mdev * mem_count
     planes = pdev * space_count
-    cell = obs_cell - lax.axis_index("space") * (pdev * slab)
-    plane = (obs_cell // slab).astype(f32)
     band = SLOTS * odev
 
     def call(*args):
@@ -495,7 +520,7 @@
     analysis = pl.pallas_call(
         call,
         out_shape=jax.ShapeDtypeStruct((pdev, mdev, slab), f32),
-        in_specs=[vmem] * 7,
+        in_specs=[vmem] * 6,
         out_specs=vmem,
         scratch_shapes=[
             pltpu.VMEM((planes, mdev // 2, 128), f32),
@@ -513,17 +538,16 @@
             pltpu.VMEM((space_count, 8, odev), f32),
             pltpu.VMEM((odev, band), bf16),
             pltpu.VMEM((odev, band), bf16),
-            pltpu.VMEM((2 * mdev, band), bf16),
-            pltpu.VMEM((2 * pdev * mdev, band), bf16),
             pltpu.SemaphoreType.DMA((SENDS,)),
             pltpu.SemaphoreType.DMA((RECVS,)),
             pltpu.SemaphoreType.DMA((3,)),
         ],
-        compiler_params=pltpu.CompilerParams(collective_id=0, has_side_effects=True),
+        compiler_params=pltpu.CompilerParams(
+            collective_id=0, has_side_effects=True, vmem_limit_bytes=32 * 1024 * 1024),
         name="cycle",
     )(
-        jnp.transpose(ensemble, (1, 0, 2)), forcing, cell[None, :], obs_value[None, :], obs_var[None, :],
-        obs_noise, plane[None, :],
+        jnp.transpose(ensemble, (1, 0, 2)), forcing, obs_cell[None, :], obs_value[None, :], obs_var[None, :],
+        obs_noise,
     )
     return jnp.transpose(analysis, (1, 0, 2))
 

time: 94.3 us -> 90.4 us (0.959)
  local copies, waits for them, and re-layouts: 5.04 us -> 3.22 us
  Pallas kernels: 88.5 us -> 87 us
    pallas_call x1, Pallas kernels: 88.5 us -> 87 us  [shards(): pl.pallas_call(call, out_shape=jax.ShapeDtypeStruct((pdev, mdev, slab), f...]
    transpose x1, local copies, waits for them, and re-layouts: 2.24 us -> 1.2 us  [shards(): return jnp.transpose(analysis, (1, 0, 2))]
    unnamed x3 -> x11, local copies, waits for them, and re-layouts: 2.8 us -> 2.02 us
where the time goes in v2:
time: 90.4 us; the launch traced here: 90.3 us
  Pallas kernels  87 us (96%)
  local copies, waits for them, and re-layouts  3.22 us (4%)
    pallas_call x1, Pallas kernels, shards(): pl.pallas_call(call, out_shape=jax.ShapeDtypeStruct((pdev, mdev, slab), f...  87 us
    unnamed x11, local copies, waits for them, and re-layouts  2.02 us

profile of v2, /device:TPU:1, one launch (start us, length us, event | category | flops | bytes accessed | tf_op | source)
XLA Modules:
  0.0 90.3 jit_solution(14814583191011788070)
XLA Ops:
  0.0 0.0 copy-start
  0.0 0.0 copy-start.1
  0.0 1.4 %copy.10 = f32[32,2,2048]{2,0,1:T(8,128)S(1)} copy(f32[32,2,2048]{2,1,0:T(2,128)} %param.6) | data formatting | bytes 1048576 | tf_op args[0]
  1.4 0.0 copy-start.2
  1.4 0.0 copy-start.3
  1.4 0.0 copy-start.4
  1.4 0.0 copy-done
  1.4 0.0 copy-done.1
  1.4 0.6 copy-done.2
  2.0 0.0 copy-done.3
  2.0 0.0 copy-done.4
  2.1 87.0 %cycle.1 = f32[2,32,2048]{2,1,0:T(8,128)S(1)} custom-call(f32[2,32,2048]{2,1,0:T(8,128)S(1)} %bitcast.8, f32[2,2048]{1,0:T(2,128)S(1)} %copy-done, s32[1,128]{1,0:T(1,128)S(1)} %bitcast.9, f32[1,128]{1,0:T(1,128)S(1)} %bitcast.10, f32[1,128]{1,0:T(1,128)S(1)} %bitcast.11, f32[32,128]{1,0:T(8,128)S(1)} %copy-done.1), custom_call_target="tpu_custom_call" | custom-call | tf_op jit(solution)/shard_map/cycle/pallas_call | solution.py:520
  89.1 1.2 %copy.8 = f32[32,2,2048]{2,1,0:T(2,128)} copy(f32[32,2,2048]{2,0,1:T(8,128)S(1)} %bitcast.7) | data formatting | bytes 1048576 | tf_op jit(solution)/shard_map/transpose | solution.py:552
Async XLA Ops:
  0.0 1.4 %copy-start = (f32[2,2048]{1,0:T(2,128)S(1)}, f32[2,2048]{1,0:T(2,128)}, u32[]{:S(2)}) copy-start(f32[2,2048]{1,0:T(2,128)} %args_1_.4) | copy-start | bytes 49156
  0.0 1.4 %copy-start.1 = (f32[32,128]{1,0:T(8,128)S(1)}, f32[32,128]{1,0:T(8,128)}, u32[]{:S(2)}) copy-start(f32[32,128]{1,0:T(8,128)} %args_5_.4) | copy-start | bytes 49156
  1.4 0.7 copy-start.2
  1.4 0.7 copy-start.3
  1.4 0.7 copy-start.4

commit v3 on v2

--- a/solution.py
+++ b/solution.py
@@ -11,15 +11,19 @@
 REACH = 8
 SLOTS = 2 * REACH + 1
 MESH = pl.DeviceIdType.MESH
+AWAY = (4, -4, 6, -6, 2, -2, 8, -8)
+STEPS = (
+    (2, 2), (2, 1), (1, 2), (2, 3), (3, 2), (1, 1), (3, 3), (1, 3),
+    (3, 1), (2, 0), (0, 2), (1, 0), (0, 1), (3, 0), (0, 3), (0, 0),
+)
 f32 = jnp.float32
 bf16 = jnp.bfloat16
 
-GROUP = 4
-GROUPS = 2 * REACH // GROUP
 HOPS = 7
-R_OUT, R_FORC, R_BACK, R_RHS, R_BOUND = range(5)
-R_DIR = 5
-R_OBS = R_DIR + GROUPS * (ITERS - 1)
+R_OUT, R_FORC, R_BACK, R_BOUND = range(4)
+R_RHS = 4
+R_DIR = R_RHS + 2 * REACH
+R_OBS = R_DIR + 2 * REACH * (ITERS - 1)
 R_BAND = R_OBS + 8
 R_RIGHT = R_BAND + SLOTS
 R_LEFT = R_RIGHT + HOPS
@@ -72,6 +76,16 @@
     def other(base, step, count):
         return lax.rem(base + step, count)
 
+    my_c, my_h = chunk_of(me_s)
+    side_y = 4
+    side_x = space_count // 2 // side_y
+    others = []
+    for dx, dy in STEPS:
+        chip = lax.rem(lax.div(my_c, side_y) + dx, side_x) * side_y + lax.rem(lax.rem(my_c, side_y) + dy, side_y)
+        others.append(2 * chip + (1 - my_h))
+        if (dx, dy) != (0, 0):
+            others.append(2 * chip + my_h)
+
     barrier = pltpu.get_barrier_semaphore()
 
     def greet_space(i, c):
@@ -85,7 +99,6 @@
     lax.fori_loop(1, space_count, greet_space, 0)
     lax.fori_loop(1, mem_count, greet_mem, 0)
 
-    my_c, my_h = chunk_of(me_s)
     own_out = pltpu.make_async_copy(
         ens.at[:, pl.ds(pl.multiple_of(my_h * half, half), half), pl.ds(pl.multiple_of(my_c * 128, 128), 128)],
         r.at[pl.ds(me_s * 2, 2)], lsem.at[0])
@@ -96,8 +109,7 @@
 
     pl.semaphore_wait(barrier, space_count + mem_count - 2)
 
-    def send_out(i, c):
-        to = other(me_s, i, space_count)
+    for to in others:
         tc, th = chunk_of(to)
         cells = pl.ds(pl.multiple_of(tc * 128, 128), 128)
         pltpu.make_async_remote_copy(
@@ -109,9 +121,6 @@
             dst_ref=r.at[pl.ds(me_s * 2, 2)],
             send_sem=ssem.at[S_OUT], recv_sem=rsem.at[R_OUT],
             device_id={"space": to}, device_id_type=MESH).start()
-        return c
-
-    lax.fori_loop(1, space_count, send_out, 0)
 
     cells_here = cell[...] - me_s * (2 * slab)
 
@@ -148,15 +157,11 @@
     my_rows = pl.ds(pl.multiple_of(me_m * mdev + my_h * half, half), half)
     my_cells = pl.ds(pl.multiple_of(my_c * 128, 128), 128)
 
-    def send_back(i, c):
-        to = other(me_s, i, space_count)
+    for to in others:
         pltpu.make_async_remote_copy(
             src_ref=r.at[pl.ds(to * 2, 2)], dst_ref=zs.at[:, my_rows, my_cells],
             send_sem=ssem.at[S_BACK], recv_sem=rsem.at[R_BACK],
             device_id={"space": to}, device_id_type=MESH).start()
-        return c
-
-    lax.fori_loop(1, space_count, send_back, 0)
     own_back = pltpu.make_async_copy(r.at[pl.ds(me_s * 2, 2)], zs.at[:, my_rows, my_cells], lsem.at[2])
     own_back.start()
     own_back.wait()
@@ -207,69 +212,78 @@
     e0[own, :mdev, :] = rhs
     e0[own, mdev:, :] = jnp.broadcast_to(plane_row, (8, odev))
 
-    def away_at(n):
-        at = lax.div(n, 2)
-        far = lax.div(at + 1, 2) * (1 - 2 * lax.rem(at + 1, 2))
-        return (REACH // 2 + far) * (1 - 2 * lax.rem(n, 2))
-
-    def place_of(away):
-        past = lax.max(away, -away) - REACH // 2
-        rank = 2 * lax.max(past, -past) - jnp.where(past > 0, 1, 0)
-        return 2 * rank + jnp.where(away < 0, 1, 0)
-
-    def band_send(src, dst_of, send, recv_of):
-        def one(i, c):
-            away = away_at(i)
-            to = lax.rem(me_s + away + space_count, space_count)
-            there = i + 1 - 2 * lax.rem(i, 2)
+    turn = 1 - 2 * my_h
+    partner = {"space": me_s + turn}
+    out_of_reach = REACH - 1 - my_h
+    band_to = [{"space": lax.rem(me_s + away + space_count, space_count)} for away in AWAY]
+
+    def spread(at, send, recv):
+        def copy(there, to):
             pltpu.make_async_remote_copy(
-                src_ref=src, dst_ref=dst_of(there),
-                send_sem=ssem.at[send], recv_sem=rsem.at[recv_of(there)],
-                device_id={"space": to}, device_id_type=MESH).start()
-            return c
-
-        lax.fori_loop(0, 2 * REACH, one, 0)
-
-    band_send(e0.at[own], lambda j: e0.at[j], S_RHS, lambda j: R_RHS)
-
-    def space_at(chips):
-        return {"space": lax.rem(me_s + 2 * chips + space_count, space_count)}
-
-    def piece_to(step, i):
-        chips = (1 + 3 * lax.div(i, 2)) * (1 - 2 * lax.rem(i, 2))
+                src_ref=at(own), dst_ref=at(there), send_sem=ssem.at[send], recv_sem=rsem.at[recv + there],
+                device_id=to, device_id_type=MESH).start()
+
+        for i, to in enumerate(band_to):
+            copy(i ^ 1, to)
+        copy(REACH + out_of_reach, partner)
+
+    def hand_over(at, send, recv):
+        def copy(i):
+            pltpu.make_async_remote_copy(
+                src_ref=at(i), dst_ref=at(REACH + i), send_sem=ssem.at[send], recv_sem=rsem.at[recv + REACH + i],
+                device_id=partner, device_id_type=MESH).start()
+
+        for i in range(REACH - 2):
+            awaited(at(i), rsem.at[recv + i])
+            copy(i)
+        for i in range(REACH - 2, REACH):
+            awaited(at(i), rsem.at[recv + i])
+        copy(2 * REACH - 3 - out_of_reach)
+
+    def handed(at, recv):
+        for i in range(REACH, 2 * REACH):
+            awaited(at(i), rsem.at[recv + i])
+
+    def rhs_at(i):
+        return e0.at[i]
+
+    spread(rhs_at, S_RHS, R_RHS)
+
+    near = (1, -1, 4, -4)
+    chips_at = {chips: {"space": lax.rem(me_s + 2 * chips + space_count, space_count)}
+                for chips in near}
+
+    def piece_rows(step):
         origin = lax.rem(me_m + mem_count - step, mem_count)
-        rows = pl.ds(pl.multiple_of(origin * mdev, mdev), mdev)
-        pltpu.make_async_remote_copy(
-            src_ref=ab.at[REACH, rows], dst_ref=ab.at[REACH - 2 * chips, rows],
-            send_sem=ssem.at[S_BAND], recv_sem=rsem.at[R_BAND + REACH - 2 * chips],
-            device_id=space_at(chips), device_id_type=MESH).start()
+        return pl.ds(pl.multiple_of(origin * mdev, mdev), mdev)
+
+    def piece_send(slot, there, rows, chips):
+        pltpu.make_async_remote_copy(
+            src_ref=ab.at[slot, rows], dst_ref=ab.at[there, rows],
+            send_sem=ssem.at[S_BAND], recv_sem=rsem.at[R_BAND + there],
+            device_id=chips_at[chips], device_id_type=MESH).start()
+
+    def to_chips(step):
+        rows = piece_rows(step)
+        for chips in near:
+            piece_send(REACH, REACH - 2 * chips, rows, chips)
 
     def piece_here(step):
         awaited(ab.at[REACH, pl.ds(0, mdev)], rsem.at[R_OBS + step])
-
-    def to_chips(step):
-        def one(i, c):
-            piece_to(step, i)
-            return c
-
-        lax.fori_loop(0, 4, one, 0)
 
     to_chips(0)
     relay(0)
     relay(1)
-    for away in range(1, mem_count // 2 + 1):
-        for step in sorted({away, mem_count - away}):
-            piece_here(step)
-            to_chips(step)
-
-    turn = 1 - 2 * my_h
-    partner = me_s + turn
+    for step in (1, 7, 2, 6, 3, 5, 4):
+        piece_here(step)
+        to_chips(step)
+    hand_over(rhs_at, S_RHS, R_RHS)
 
     def pair_send(e):
         pltpu.make_async_remote_copy(
             src_ref=ab.at[REACH + turn * e], dst_ref=ab.at[REACH + turn * (e - 1)],
             send_sem=ssem.at[S_PAIR], recv_sem=rsem.at[R_BAND + REACH + turn * (e - 1)],
-            device_id={"space": partner}, device_id_type=MESH).start()
+            device_id=partner, device_id_type=MESH).start()
 
     def slot_here(j):
         awaited(ab.at[0], rsem.at[R_BAND + j])
@@ -293,7 +307,8 @@
         spread = jnp.minimum(spread, planes - spread)
         return jnp.maximum(0.0, 1.0 - spread / LOC)
 
-    def rows_of(j, place, total, more=None):
+    def rows_of(j, place, carry, more=None):
+        total, image = carry
         lanes = pl.ds(pl.multiple_of(place * odev, odev), odev)
         high, low = halves(anomalies(j))
         ah[:, lanes] = high
@@ -306,35 +321,22 @@
         chigh, clow = halves(block)
         ch[:, lanes] = chigh
         cl[:, lanes] = clow
-        return total + jnp.abs(block)
-
-    total = rows_of(REACH, own, jnp.zeros((odev, odev), f32), diag_var)
+        dhigh, dlow = halves(e0[place, pl.ds(0, mdev), :])
+        top = nt(jnp.concatenate([dhigh, dlow], axis=0), chigh)
+        return total + jnp.abs(block), image + (top[:mdev] + top[mdev:] + nt(dhigh, clow))
+
+    total = rows_of(REACH, own, (jnp.zeros((odev, odev), f32), jnp.zeros((mdev, odev), f32)), diag_var)
 
     for side in (1, -1):
         slot = REACH + 2 * side
         slot_here(slot)
         for chips in (-side, 4 * side):
-            there = REACH + 2 * (side - chips)
-            pltpu.make_async_remote_copy(
-                src_ref=ab.at[slot], dst_ref=ab.at[there],
-                send_sem=ssem.at[S_BAND], recv_sem=rsem.at[R_BAND + there],
-                device_id=space_at(chips), device_id_type=MESH).start()
+            piece_send(slot, slot - 2 * chips, slice(None), chips)
     pair_send(2)
     pair_send(-2)
-    awaited(e0.at[pl.ds(0, 2 * REACH)], rsem.at[R_RHS])
-
-    def slot_rows(e, total):
-        return rows_of(REACH + turn * e, place_of(turn * e), total)
-
-    def from_partner(e, total):
-        slot_here(REACH + turn * (1 - e))
-        return slot_rows(1 - e, total)
-
-    total = slot_rows(2, total)
-    total = slot_rows(-2, total)
-    total = from_partner(0, total)
     relayed(0)
     relay(2)
+    handed(rhs_at, R_RHS)
 
     def pick(i, table):
         value = table[0]
@@ -342,55 +344,75 @@
             value = jnp.where(i == k, table[k], value)
         return value
 
+    def place(rank, negative):
+        return 2 * rank + my_h + negative - 2 * my_h * negative
+
+    def slot_rows(e, rank, negative, total):
+        return rows_of(REACH + turn * e, place(rank, negative), total)
+
+    def from_partner(e, rank, negative, total):
+        slot_here(REACH + turn * (1 - e))
+        return rows_of(REACH + turn * (1 - e), REACH + place(rank, 1 - negative), total)
+
+    total = slot_rows(2, 2, 0, total)
+    total = slot_rows(-2, 2, 1, total)
+    total = from_partner(0, 3, 1, total)
+
     def two_slots(i, total):
         e = pick(i, (8, 4, -4, 6, -6))
         slot_here(REACH + turn * e)
         pair_send(e)
-        total = slot_rows(e, total)
-        return from_partner(pick(i, (2, -2, 8, 4, -4)), total)
-
-    total = lax.fori_loop(0, 5, two_slots, total)
-    slot_here(REACH - turn * REACH)
-    total = slot_rows(-REACH, total)
-
-    def last_two(i, total):
-        return from_partner(pick(i, (6, -6)), total)
-
-    total = lax.fori_loop(0, 2, last_two, total)
+        total = slot_rows(e, pick(i, (3, 0, 0, 1, 1)), pick(i, (0, 0, 1, 0, 1)), total)
+        return from_partner(
+            pick(i, (2, -2, 8, 4, -4)), pick(i, (2, 2, 3, 0, 0)), pick(i, (0, 1, 0, 0, 1)), total)
+
+    total = lax.fori_loop(0, 2, two_slots, total)
     relayed(1)
     relay(3)
+    total = lax.fori_loop(2, 5, two_slots, total)
+    slot_here(REACH - turn * REACH)
+    total = slot_rows(-REACH, 3, 1, total)
+
+    def last_two(i, total):
+        return from_partner(pick(i, (6, -6)), 1, i, total)
+
+    total, first_image = lax.fori_loop(0, 2, last_two, total)
 
     def part(block, lanes):
         high, low = halves(block)
         top = nt(jnp.concatenate([high, low], axis=0), ch[:, lanes])
         return top[:mdev] + top[mdev:] + nt(high, cl[:, lanes])
 
+    own_lanes = slice(own * odev, (own + 1) * odev)
+    halves_of_band = ((0, REACH), (REACH, 2 * REACH))
+
+    def at_of(e):
+        return lambda i: ex.at[e, i]
+
+    def exchange(e, block):
+        ex[e, own] = block
+        spread(at_of(e), S_DIR + e, R_DIR + 2 * REACH * e)
+
+    def arrived(e):
+        def group(g):
+            recv = R_DIR + 2 * REACH * e
+            if g == 0:
+                hand_over(at_of(e), S_DIR + e, recv)
+            else:
+                handed(at_of(e), recv)
+            return jnp.concatenate([ex[e, i] for i in range(*halves_of_band[g])], axis=1)
+
+        return group
+
     def lanes_of(g):
-        return slice(g * GROUP * odev, (g + 1) * GROUP * odev)
-
-    own_lanes = slice(own * odev, (own + 1) * odev)
+        return slice(halves_of_band[g][0] * odev, halves_of_band[g][1] * odev)
 
     def image_of(block, group):
         image = part(block, own_lanes)
-        for g in range(GROUPS):
+        for g in range(2):
             image = image + part(group(g), lanes_of(g))
         return image
 
-    def rhs_group(g):
-        return jnp.concatenate([e0[g * GROUP + k, :mdev, :] for k in range(GROUP)], axis=1)
-
-    def exchange(e, block):
-        ex[e, own] = block
-        band_send(ex.at[e, own], lambda j: ex.at[e, j], S_DIR + e, lambda j: R_DIR + GROUPS * e + lax.div(j, GROUP))
-
-    def arrived(e):
-        def group(g):
-            awaited(ex.at[e, pl.ds(g * GROUP, GROUP)], rsem.at[R_DIR + GROUPS * e + g])
-            return jnp.concatenate([ex[e, g * GROUP + k] for k in range(GROUP)], axis=1)
-
-        return group
-
-    first_image = image_of(rhs, rhs_group)
     exchange(0, first_image)
 
     row_max = jnp.max(jnp.sum(total, axis=1, keepdims=True), axis=0, keepdims=True)
@@ -398,18 +420,17 @@
     is_upper = lax.broadcasted_iota(jnp.int32, (8, odev), 0) < 4
     bb[me_s] = jnp.where(is_upper, row_max, -var_min)
 
-    def send_bound(i, c):
+    for to in others:
         pltpu.make_async_remote_copy(
             src_ref=bb.at[me_s], dst_ref=bb.at[me_s],
             send_sem=ssem.at[S_BOUND], recv_sem=rsem.at[R_BOUND],
-            device_id={"space": other(me_s, i, space_count)}, device_id_type=MESH).start()
-        return c
-
-    lax.fori_loop(1, space_count, send_bound, 0)
-
-    second_image = image_of(first_image, arrived(0))
+            device_id={"space": to}, device_id_type=MESH).start()
     relayed(2)
     relay(4)
+
+    second_image = image_of(first_image, arrived(0))
+    relayed(3)
+    relay(5)
 
     awaited(bb.at[pl.ds(0, space_count - 1)], rsem.at[R_BOUND])
     bounds = jnp.max(bb[...], axis=0)
@@ -437,9 +458,9 @@
         weight = weight + direction
         exchange(e, direction)
         image = image_of(direction, arrived(e))
-        if e < 3:
-            relayed(e + 2)
-            relay(e + 4)
+        if e == 1:
+            relayed(4)
+            relay(6)
     residual = residual - image
     rho_next = 1.0 / (2.0 * sigma - rho)
     direction = rho_next * rho * direction + 2.0 * rho_next / radius * residual
@@ -472,8 +493,8 @@
 
     gain = gain_part(weight, plane_row, own_lanes)
     group = arrived(last)
-    for g in range(GROUPS):
-        rows = jnp.concatenate([e0[g * GROUP + k, pl.ds(mdev, 1), :] for k in range(GROUP)], axis=1)
+    for g in range(2):
+        rows = jnp.concatenate([e0[i, pl.ds(mdev, 1), :] for i in range(*halves_of_band[g])], axis=1)
         gain = gain + gain_part(group(g), rows, lanes_of(g))
     gain = gain / (members - 1)
 

time: 90.4 us -> 89.5 us (0.990)
  no operation moved by 1% of the time
where the time goes in v3:
time: 89.5 us; the launch traced here: 89.4 us
  Pallas kernels  86.2 us (96%)
  local copies, waits for them, and re-layouts  3.22 us (4%)
    pallas_call x1, Pallas kernels, shards(): pl.pallas_call(call, out_shape=jax.ShapeDtypeStruct((pdev, mdev, slab), f...  86.2 us
    unnamed x11, local copies, waits for them, and re-layouts  2.02 us

profile of v3, /device:TPU:1, one launch (start us, length us, event | category | flops | bytes accessed | tf_op | source)
XLA Modules:
  0.0 89.4 jit_solution(6219659130382876426)
XLA Ops:
  0.0 0.0 copy-start
  0.0 0.0 copy-start.1
  0.0 1.4 %copy.10 = f32[32,2,2048]{2,0,1:T(8,128)S(1)} copy(f32[32,2,2048]{2,1,0:T(2,128)} %param.6) | data formatting | bytes 1048576 | tf_op args[0]
  1.4 0.0 copy-start.2
  1.4 0.0 copy-start.3
  1.4 0.0 copy-start.4
  1.4 0.0 copy-done
  1.4 0.0 copy-done.1
  1.4 0.6 copy-done.2
  2.0 0.0 copy-done.3
  2.0 0.0 copy-done.4
  2.1 86.2 %cycle.1 = f32[2,32,2048]{2,1,0:T(8,128)S(1)} custom-call(f32[2,32,2048]{2,1,0:T(8,128)S(1)} %bitcast.8, f32[2,2048]{1,0:T(2,128)S(1)} %copy-done, s32[1,128]{1,0:T(1,128)S(1)} %bitcast.9, f32[1,128]{1,0:T(1,128)S(1)} %bitcast.10, f32[1,128]{1,0:T(1,128)S(1)} %bitcast.11, f32[32,128]{1,0:T(8,128)S(1)} %copy-done.1), custom_call_target="tpu_custom_call" | custom-call | tf_op jit(solution)/shard_map/cycle/pallas_call | solution.py:541
  88.2 1.2 %copy.8 = f32[32,2,2048]{2,1,0:T(2,128)} copy(f32[32,2,2048]{2,0,1:T(8,128)S(1)} %bitcast.7) | data formatting | bytes 1048576 | tf_op jit(solution)/shard_map/transpose | solution.py:573
Async XLA Ops:
  0.0 1.4 %copy-start = (f32[2,2048]{1,0:T(2,128)S(1)}, f32[2,2048]{1,0:T(2,128)}, u32[]{:S(2)}) copy-start(f32[2,2048]{1,0:T(2,128)} %args_1_.4) | copy-start | bytes 49156
  0.0 1.4 %copy-start.1 = (f32[32,128]{1,0:T(8,128)S(1)}, f32[32,128]{1,0:T(8,128)}, u32[]{:S(2)}) copy-start(f32[32,128]{1,0:T(8,128)} %args_5_.4) | copy-start | bytes 49156
  1.4 0.7 copy-start.2
  1.4 0.7 copy-start.3
  1.4 0.7 copy-start.4

commit v4 on v3

--- a/solution.py
+++ b/solution.py
@@ -23,7 +23,7 @@
 R_OUT, R_FORC, R_BACK, R_BOUND = range(4)
 R_RHS = 4
 R_DIR = R_RHS + 2 * REACH
-R_OBS = R_DIR + 2 * REACH * (ITERS - 1)
+R_OBS = R_DIR + ITERS - 1
 R_BAND = R_OBS + 8
 R_RIGHT = R_BAND + SLOTS
 R_LEFT = R_RIGHT + HOPS
@@ -58,7 +58,7 @@
     space_count, mem_count,
     ens, forc, cell, value, var, noise,
     out,
-    r, t, fr, zs, sh, sl, oh, ab, ah, al, e0, ex, bb, ch, cl,
+    r, t, fr, zs, sh, sl, oh, ab, ah, al, e0, ex, bb, ch, cl, dh,
     ssem, rsem, lsem,
 ):
     me_s = lax.axis_index("space")
@@ -307,8 +307,7 @@
         spread = jnp.minimum(spread, planes - spread)
         return jnp.maximum(0.0, 1.0 - spread / LOC)
 
-    def rows_of(j, place, carry, more=None):
-        total, image = carry
+    def rows_of(j, place, total, more=None):
         lanes = pl.ds(pl.multiple_of(place * odev, odev), odev)
         high, low = halves(anomalies(j))
         ah[:, lanes] = high
@@ -321,11 +320,9 @@
         chigh, clow = halves(block)
         ch[:, lanes] = chigh
         cl[:, lanes] = clow
-        dhigh, dlow = halves(e0[place, pl.ds(0, mdev), :])
-        top = nt(jnp.concatenate([dhigh, dlow], axis=0), chigh)
-        return total + jnp.abs(block), image + (top[:mdev] + top[mdev:] + nt(dhigh, clow))
-
-    total = rows_of(REACH, own, (jnp.zeros((odev, odev), f32), jnp.zeros((mdev, odev), f32)), diag_var)
+        return total + jnp.abs(block)
+
+    total = rows_of(REACH, own, jnp.zeros((odev, odev), f32), diag_var)
 
     for side in (1, -1):
         slot = REACH + 2 * side
@@ -334,8 +331,6 @@
             piece_send(slot, slot - 2 * chips, slice(None), chips)
     pair_send(2)
     pair_send(-2)
-    relayed(0)
-    relay(2)
     handed(rhs_at, R_RHS)
 
     def pick(i, table):
@@ -350,33 +345,34 @@
     def slot_rows(e, rank, negative, total):
         return rows_of(REACH + turn * e, place(rank, negative), total)
 
-    def from_partner(e, rank, negative, total):
-        slot_here(REACH + turn * (1 - e))
+    def partner_rows(e, rank, negative, total):
         return rows_of(REACH + turn * (1 - e), REACH + place(rank, 1 - negative), total)
 
     total = slot_rows(2, 2, 0, total)
     total = slot_rows(-2, 2, 1, total)
-    total = from_partner(0, 3, 1, total)
 
     def two_slots(i, total):
         e = pick(i, (8, 4, -4, 6, -6))
+        f = pick(i, (0, 2, -2, 8, 4))
         slot_here(REACH + turn * e)
         pair_send(e)
+        slot_here(REACH + turn * (1 - f))
         total = slot_rows(e, pick(i, (3, 0, 0, 1, 1)), pick(i, (0, 0, 1, 0, 1)), total)
-        return from_partner(
-            pick(i, (2, -2, 8, 4, -4)), pick(i, (2, 2, 3, 0, 0)), pick(i, (0, 1, 0, 0, 1)), total)
-
-    total = lax.fori_loop(0, 2, two_slots, total)
-    relayed(1)
-    relay(3)
-    total = lax.fori_loop(2, 5, two_slots, total)
+        return partner_rows(f, pick(i, (3, 2, 2, 3, 0)), pick(i, (1, 0, 1, 0, 0)), total)
+
+    total = lax.fori_loop(0, 1, two_slots, total)
+    for hop in (0, 1):
+        relayed(hop)
+        relay(hop + 2)
+    total = lax.fori_loop(1, 5, two_slots, total)
     slot_here(REACH - turn * REACH)
+    slot_here(REACH + turn * (1 + 4))
     total = slot_rows(-REACH, 3, 1, total)
-
-    def last_two(i, total):
-        return from_partner(pick(i, (6, -6)), 1, i, total)
-
-    total, first_image = lax.fori_loop(0, 2, last_two, total)
+    total = partner_rows(-4, 0, 1, total)
+    slot_here(REACH + turn * (1 - 6))
+    slot_here(REACH + turn * (1 + 6))
+    total = partner_rows(6, 1, 0, total)
+    total = partner_rows(-6, 1, 1, total)
 
     def part(block, lanes):
         high, low = halves(block)
@@ -384,36 +380,38 @@
         return top[:mdev] + top[mdev:] + nt(high, cl[:, lanes])
 
     own_lanes = slice(own * odev, (own + 1) * odev)
-    halves_of_band = ((0, REACH), (REACH, 2 * REACH))
-
-    def at_of(e):
-        return lambda i: ex.at[e, i]
+    lanes_out = slice(0, own * odev)
 
     def exchange(e, block):
         ex[e, own] = block
-        spread(at_of(e), S_DIR + e, R_DIR + 2 * REACH * e)
+
+        def copy(there, to):
+            pltpu.make_async_remote_copy(
+                src_ref=ex.at[e, own], dst_ref=ex.at[e, there],
+                send_sem=ssem.at[S_DIR + e], recv_sem=rsem.at[R_DIR + e],
+                device_id=to, device_id_type=MESH).start()
+
+        for i, to in enumerate(band_to):
+            copy(i ^ 1, to)
+            if i < REACH - 2:
+                copy(REACH + (i ^ 1), {"space": lax.rem(me_s + AWAY[i] + turn + space_count, space_count)})
+        copy(3 * REACH - 3 - out_of_reach,
+             {"space": lax.rem(me_s - (REACH - 1) * turn + space_count, space_count)})
+        copy(REACH + out_of_reach, partner)
 
     def arrived(e):
-        def group(g):
-            recv = R_DIR + 2 * REACH * e
-            if g == 0:
-                hand_over(at_of(e), S_DIR + e, recv)
-            else:
-                handed(at_of(e), recv)
-            return jnp.concatenate([ex[e, i] for i in range(*halves_of_band[g])], axis=1)
-
-        return group
-
-    def lanes_of(g):
-        return slice(halves_of_band[g][0] * odev, halves_of_band[g][1] * odev)
-
-    def image_of(block, group):
+        awaited(ex.at[e, pl.ds(0, own)], rsem.at[R_DIR + e])
+        return lambda i: ex[e, i]
+
+    def image_of(block, values_of):
         image = part(block, own_lanes)
-        for g in range(2):
-            image = image + part(group(g), lanes_of(g))
-        return image
-
-    exchange(0, first_image)
+        values = values_of()
+        for i in range(own):
+            high, low = halves(values(i))
+            dh[:mdev, i * odev:(i + 1) * odev] = high
+            dh[mdev:, i * odev:(i + 1) * odev] = low
+        top = nt(dh[...], ch[:, lanes_out])
+        return image + (top[:mdev] + top[mdev:] + nt(dh[:mdev, :], cl[:, lanes_out]))
 
     row_max = jnp.max(jnp.sum(total, axis=1, keepdims=True), axis=0, keepdims=True)
     var_min = jnp.min(var[...], axis=1, keepdims=True)
@@ -425,12 +423,10 @@
             src_ref=bb.at[me_s], dst_ref=bb.at[me_s],
             send_sem=ssem.at[S_BOUND], recv_sem=rsem.at[R_BOUND],
             device_id={"space": to}, device_id_type=MESH).start()
-    relayed(2)
-    relay(4)
-
-    second_image = image_of(first_image, arrived(0))
-    relayed(3)
-    relay(5)
+
+    first_image = image_of(rhs, lambda: lambda i: e0[i, pl.ds(0, mdev), :])
+    exchange(0, first_image)
+    second_image = image_of(first_image, lambda: arrived(0))
 
     awaited(bb.at[pl.ds(0, space_count - 1)], rsem.at[R_BOUND])
     bounds = jnp.max(bb[...], axis=0)
@@ -457,10 +453,14 @@
         rho = rho_next
         weight = weight + direction
         exchange(e, direction)
-        image = image_of(direction, arrived(e))
         if e == 1:
+            for hop in (2, 3):
+                relayed(hop)
+                relay(hop + 2)
+        if e == 3:
             relayed(4)
             relay(6)
+        image = image_of(direction, lambda e=e: arrived(e))
     residual = residual - image
     rho_next = 1.0 / (2.0 * sigma - rho)
     direction = rho_next * rho * direction + 2.0 * rho_next / radius * residual
@@ -492,10 +492,12 @@
         return top[:2 * mdev] + top[2 * mdev:] + nt(high, al[:, lanes])
 
     gain = gain_part(weight, plane_row, own_lanes)
-    group = arrived(last)
-    for g in range(2):
-        rows = jnp.concatenate([e0[i, pl.ds(mdev, 1), :] for i in range(*halves_of_band[g])], axis=1)
-        gain = gain + gain_part(group(g), rows, lanes_of(g))
+    values = arrived(last)
+    for g in (slice(0, REACH), slice(REACH, own)):
+        span = range(g.start, g.stop)
+        rows = jnp.concatenate([e0[i, pl.ds(mdev, 1), :] for i in span], axis=1)
+        block = jnp.concatenate([values(i) for i in span], axis=1)
+        gain = gain + gain_part(block, rows, slice(g.start * odev, g.stop * odev))
     gain = gain / (members - 1)
 
     for x in range(2):
@@ -559,6 +561,7 @@
             pltpu.VMEM((space_count, 8, odev), f32),
             pltpu.VMEM((odev, band), bf16),
             pltpu.VMEM((odev, band), bf16),
+            pltpu.VMEM((2 * mdev, 2 * REACH * odev), bf16),
             pltpu.SemaphoreType.DMA((SENDS,)),
             pltpu.SemaphoreType.DMA((RECVS,)),
             pltpu.SemaphoreType.DMA((3,)),

time: 89.5 us -> 89.2 us (level)
  no operation moved by 1% of the time
where the time goes in v4:
time: 89.2 us; the launch traced here: 89.1 us
  Pallas kernels  85.8 us (96%)
  local copies, waits for them, and re-layouts  3.22 us (4%)
    pallas_call x1, Pallas kernels, shards(): pl.pallas_call(call, out_shape=jax.ShapeDtypeStruct((pdev, mdev, slab), f...  85.8 us
    unnamed x11, local copies, waits for them, and re-layouts  2.02 us

profile of v4, /device:TPU:1, one launch (start us, length us, event | category | flops | bytes accessed | tf_op | source)
XLA Modules:
  0.0 89.1 jit_solution(8169810706312377203)
XLA Ops:
  0.0 0.0 copy-start
  0.0 0.0 copy-start.1
  0.0 1.4 %copy.10 = f32[32,2,2048]{2,0,1:T(8,128)S(1)} copy(f32[32,2,2048]{2,1,0:T(2,128)} %param.6) | data formatting | bytes 1048576 | tf_op args[0]
  1.4 0.0 copy-start.2
  1.4 0.0 copy-start.3
  1.4 0.0 copy-start.4
  1.4 0.0 copy-done
  1.4 0.0 copy-done.1
  1.4 0.6 copy-done.2
  2.0 0.0 copy-done.3
  2.0 0.0 copy-done.4
  2.1 85.8 %cycle.1 = f32[2,32,2048]{2,1,0:T(8,128)S(1)} custom-call(f32[2,32,2048]{2,1,0:T(8,128)S(1)} %bitcast.8, f32[2,2048]{1,0:T(2,128)S(1)} %copy-done, s32[1,128]{1,0:T(1,128)S(1)} %bitcast.9, f32[1,128]{1,0:T(1,128)S(1)} %bitcast.10, f32[1,128]{1,0:T(1,128)S(1)} %bitcast.11, f32[32,128]{1,0:T(8,128)S(1)} %copy-done.1), custom_call_target="tpu_custom_call" | custom-call | tf_op jit(solution)/shard_map/cycle/pallas_call | solution.py:543
  87.9 1.2 %copy.8 = f32[32,2,2048]{2,1,0:T(2,128)} copy(f32[32,2,2048]{2,0,1:T(8,128)S(1)} %bitcast.7) | data formatting | bytes 1048576 | tf_op jit(solution)/shard_map/transpose | solution.py:576
Async XLA Ops:
  0.0 1.4 %copy-start = (f32[2,2048]{1,0:T(2,128)S(1)}, f32[2,2048]{1,0:T(2,128)}, u32[]{:S(2)}) copy-start(f32[2,2048]{1,0:T(2,128)} %args_1_.4) | copy-start | bytes 49156
  0.0 1.4 %copy-start.1 = (f32[32,128]{1,0:T(8,128)S(1)}, f32[32,128]{1,0:T(8,128)}, u32[]{:S(2)}) copy-start(f32[32,128]{1,0:T(8,128)} %args_5_.4) | copy-start | bytes 49156
  1.4 0.7 copy-start.2
  1.4 0.7 copy-start.3
  1.4 0.7 copy-start.4

commit v5 on v4

--- a/solution.py
+++ b/solution.py
@@ -361,9 +361,8 @@
         return partner_rows(f, pick(i, (3, 2, 2, 3, 0)), pick(i, (1, 0, 1, 0, 0)), total)
 
     total = lax.fori_loop(0, 1, two_slots, total)
-    for hop in (0, 1):
-        relayed(hop)
-        relay(hop + 2)
+    relayed(0)
+    relay(2)
     total = lax.fori_loop(1, 5, two_slots, total)
     slot_here(REACH - turn * REACH)
     slot_here(REACH + turn * (1 + 4))
@@ -426,6 +425,8 @@
 
     first_image = image_of(rhs, lambda: lambda i: e0[i, pl.ds(0, mdev), :])
     exchange(0, first_image)
+    relayed(1)
+    relay(3)
     second_image = image_of(first_image, lambda: arrived(0))
 
     awaited(bb.at[pl.ds(0, space_count - 1)], rsem.at[R_BOUND])
@@ -453,13 +454,8 @@
         rho = rho_next
         weight = weight + direction
         exchange(e, direction)
-        if e == 1:
-            for hop in (2, 3):
-                relayed(hop)
-                relay(hop + 2)
-        if e == 3:
-            relayed(4)
-            relay(6)
+        relayed(e + 1)
+        relay(e + 3)
         image = image_of(direction, lambda e=e: arrived(e))
     residual = residual - image
     rho_next = 1.0 / (2.0 * sigma - rho)
@@ -504,13 +500,15 @@
         ghigh, glow = halves(gain[x * mdev:(x + 1) * mdev])
         gboth = jnp.concatenate([ghigh, glow], axis=0)
 
+        wide = 1024
+
         def update(i, c, x=x, ghigh=ghigh, gboth=gboth):
-            lanes = pl.ds(pl.multiple_of(i * width, width), width)
+            lanes = pl.ds(pl.multiple_of(i * wide, wide), wide)
             top = nn(gboth, sh[x, :, lanes])
             out[x, :, lanes] = zs[x, mine, lanes] + (top[:mdev] + top[mdev:] + nn(ghigh, sl[x, :, lanes]))
             return c
 
-        lax.fori_loop(0, slab // width, update, 0)
+        lax.fori_loop(0, slab // wide, update, 0)
 
     awaited(r.at[pl.ds(0, planes - 2)], ssem.at[S_OUT])
     awaited(fr.at[pl.ds(0, space_count - 1)], ssem.at[S_FORC])

time: 89.2 us -> 88.7 us (level)
  no operation moved by 1% of the time
where the time goes in v5:
time: 88.7 us; the launch traced here: 88.6 us
  Pallas kernels  85.3 us (96%)
  local copies, waits for them, and re-layouts  3.22 us (4%)
    pallas_call x1, Pallas kernels, shards(): pl.pallas_call(call, out_shape=jax.ShapeDtypeStruct((pdev, mdev, slab), f...  85.3 us
    unnamed x11, local copies, waits for them, and re-layouts  2.02 us

profile of v5, /device:TPU:1, one launch (start us, length us, event | category | flops | bytes accessed | tf_op | source)
XLA Modules:
  0.0 88.6 jit_solution(10270430925872822788)
XLA Ops:
  0.0 0.0 copy-start
  0.0 0.0 copy-start.1
  0.0 1.4 %copy.10 = f32[32,2,2048]{2,0,1:T(8,128)S(1)} copy(f32[32,2,2048]{2,1,0:T(2,128)} %param.6) | data formatting | bytes 1048576 | tf_op args[0]
  1.4 0.0 copy-start.2
  1.4 0.0 copy-start.3
  1.4 0.0 copy-start.4
  1.4 0.0 copy-done
  1.4 0.0 copy-done.1
  1.4 0.6 copy-done.2
  2.0 0.0 copy-done.3
  2.0 0.0 copy-done.4
  2.1 85.3 %cycle.1 = f32[2,32,2048]{2,1,0:T(8,128)S(1)} custom-call(f32[2,32,2048]{2,1,0:T(8,128)S(1)} %bitcast.8, f32[2,2048]{1,0:T(2,128)S(1)} %copy-done, s32[1,128]{1,0:T(1,128)S(1)} %bitcast.9, f32[1,128]{1,0:T(1,128)S(1)} %bitcast.10, f32[1,128]{1,0:T(1,128)S(1)} %bitcast.11, f32[32,128]{1,0:T(8,128)S(1)} %copy-done.1), custom_call_target="tpu_custom_call" | custom-call | tf_op jit(solution)/shard_map/cycle/pallas_call | solution.py:541
  87.4 1.2 %copy.8 = f32[32,2,2048]{2,1,0:T(2,128)} copy(f32[32,2,2048]{2,0,1:T(8,128)S(1)} %bitcast.7) | data formatting | bytes 1048576 | tf_op jit(solution)/shard_map/transpose | solution.py:574
Async XLA Ops:
  0.0 1.4 %copy-start = (f32[2,2048]{1,0:T(2,128)S(1)}, f32[2,2048]{1,0:T(2,128)}, u32[]{:S(2)}) copy-start(f32[2,2048]{1,0:T(2,128)} %args_1_.4) | copy-start | bytes 49156
  0.0 1.4 %copy-start.1 = (f32[32,128]{1,0:T(8,128)S(1)}, f32[32,128]{1,0:T(8,128)}, u32[]{:S(2)}) copy-start(f32[32,128]{1,0:T(8,128)} %args_5_.4) | copy-start | bytes 49156
  1.4 0.7 copy-start.2
  1.4 0.7 copy-start.3
  1.4 0.7 copy-start.4

commit v6 on v5

--- a/solution.py
+++ b/solution.py
@@ -327,8 +327,15 @@
     for side in (1, -1):
         slot = REACH + 2 * side
         slot_here(slot)
-        for chips in (-side, 4 * side):
-            piece_send(slot, slot - 2 * chips, slice(None), chips)
+        piece_send(slot, slot + 2 * side, slice(None), -side)
+        edge = lax.rem(my_c, side_y) == (side_y - 1 if side > 0 else 0)
+        given = jnp.where(edge, REACH, slot)
+        chips = jnp.where(edge, -3 * side, 4 * side)
+        there = given - 2 * chips
+        pltpu.make_async_remote_copy(
+            src_ref=ab.at[given], dst_ref=ab.at[there],
+            send_sem=ssem.at[S_BAND], recv_sem=rsem.at[R_BAND + there],
+            device_id={"space": lax.rem(me_s + 2 * chips + space_count, space_count)}, device_id_type=MESH).start()
     pair_send(2)
     pair_send(-2)
     handed(rhs_at, R_RHS)

time: 88.7 us -> 87.6 us (0.988)
  Pallas kernels: 85.3 us -> 84.2 us
    pallas_call x1, Pallas kernels: 85.3 us -> 84.2 us  [shards(): pl.pallas_call(call, out_shape=jax.ShapeDtypeStruct((pdev, mdev, slab), f...]
where the time goes in v6:
time: 87.6 us; the launch traced here: 87.5 us
  Pallas kernels  84.2 us (96%)
  local copies, waits for them, and re-layouts  3.22 us (4%)
    pallas_call x1, Pallas kernels, shards(): pl.pallas_call(call, out_shape=jax.ShapeDtypeStruct((pdev, mdev, slab), f...  84.2 us
    unnamed x11, local copies, waits for them, and re-layouts  2.02 us

profile of v6, /device:TPU:1, one launch (start us, length us, event | category | flops | bytes accessed | tf_op | source)
XLA Modules:
  0.0 87.5 jit_solution(17425841882132134684)
XLA Ops:
  0.0 0.0 copy-start
  0.0 0.0 copy-start.1
  0.0 1.4 %copy.10 = f32[32,2,2048]{2,0,1:T(8,128)S(1)} copy(f32[32,2,2048]{2,1,0:T(2,128)} %param.6) | data formatting | bytes 1048576 | tf_op args[0]
  1.4 0.0 copy-start.2
  1.4 0.0 copy-start.3
  1.4 0.0 copy-start.4
  1.4 0.0 copy-done
  1.4 0.0 copy-done.1
  1.4 0.6 copy-done.2
  2.0 0.0 copy-done.3
  2.0 0.0 copy-done.4
  2.1 84.2 %cycle.1 = f32[2,32,2048]{2,1,0:T(8,128)S(1)} custom-call(f32[2,32,2048]{2,1,0:T(8,128)S(1)} %bitcast.8, f32[2,2048]{1,0:T(2,128)S(1)} %copy-done, s32[1,128]{1,0:T(1,128)S(1)} %bitcast.9, f32[1,128]{1,0:T(1,128)S(1)} %bitcast.10, f32[1,128]{1,0:T(1,128)S(1)} %bitcast.11, f32[32,128]{1,0:T(8,128)S(1)} %copy-done.1), custom_call_target="tpu_custom_call" | custom-call | tf_op jit(solution)/shard_map/cycle/pallas_call | solution.py:548
  86.3 1.2 %copy.8 = f32[32,2,2048]{2,1,0:T(2,128)} copy(f32[32,2,2048]{2,0,1:T(8,128)S(1)} %bitcast.7) | data formatting | bytes 1048576 | tf_op jit(solution)/shard_map/transpose | solution.py:581
Async XLA Ops:
  0.0 1.4 %copy-start = (f32[2,2048]{1,0:T(2,128)S(1)}, f32[2,2048]{1,0:T(2,128)}, u32[]{:S(2)}) copy-start(f32[2,2048]{1,0:T(2,128)} %args_1_.4) | copy-start | bytes 49156
  0.0 1.4 %copy-start.1 = (f32[32,128]{1,0:T(8,128)S(1)}, f32[32,128]{1,0:T(8,128)}, u32[]{:S(2)}) copy-start(f32[32,128]{1,0:T(8,128)} %args_5_.4) | copy-start | bytes 49156
  1.4 0.7 copy-start.2
  1.4 0.7 copy-start.3
  1.4 0.7 copy-start.4

commit v7 on v5

--- a/solution.py
+++ b/solution.py
@@ -324,11 +324,21 @@
 
     total = rows_of(REACH, own, jnp.zeros((odev, odev), f32), diag_var)
 
-    for side in (1, -1):
+    def pass_on(given, chips):
+        there = given - 2 * chips
+        pltpu.make_async_remote_copy(
+            src_ref=ab.at[given], dst_ref=ab.at[there],
+            send_sem=ssem.at[S_BAND], recv_sem=rsem.at[R_BAND + there],
+            device_id={"space": lax.rem(me_s + 2 * chips + space_count, space_count)}, device_id_type=MESH).start()
+
+    my_y = lax.rem(my_c, side_y)
+    first_side = jnp.where(my_y == side_y - 1, -1, 1)
+    for side in (first_side, -first_side):
         slot = REACH + 2 * side
         slot_here(slot)
-        for chips in (-side, 4 * side):
-            piece_send(slot, slot - 2 * chips, slice(None), chips)
+        pass_on(slot, -side)
+        edge = my_y == jnp.where(side > 0, side_y - 1, 0)
+        pass_on(jnp.where(edge, REACH, slot), jnp.where(edge, -3 * side, 4 * side))
     pair_send(2)
     pair_send(-2)
     handed(rhs_at, R_RHS)

time: 88.7 us -> 87.2 us (0.983)
  Pallas kernels: 85.3 us -> 83.8 us
    pallas_call x1, Pallas kernels: 85.3 us -> 83.8 us  [shards(): pl.pallas_call(call, out_shape=jax.ShapeDtypeStruct((pdev, mdev, slab), f...]
where the time goes in v7:
time: 87.2 us; the launch traced here: 87.1 us
  Pallas kernels  83.8 us (96%)
  local copies, waits for them, and re-layouts  3.22 us (4%)
    pallas_call x1, Pallas kernels, shards(): pl.pallas_call(call, out_shape=jax.ShapeDtypeStruct((pdev, mdev, slab), f...  83.8 us
    unnamed x11, local copies, waits for them, and re-layouts  2.02 us

profile of v7, /device:TPU:1, one launch (start us, length us, event | category | flops | bytes accessed | tf_op | source)
XLA Modules:
  0.0 87.1 jit_solution(12422726855445176163)
XLA Ops:
  0.0 0.0 copy-start
  0.0 0.0 copy-start.1
  0.0 1.4 %copy.10 = f32[32,2,2048]{2,0,1:T(8,128)S(1)} copy(f32[32,2,2048]{2,1,0:T(2,128)} %param.6) | data formatting | bytes 1048576 | tf_op args[0]
  1.4 0.0 copy-start.2
  1.4 0.0 copy-start.3
  1.4 0.0 copy-start.4
  1.4 0.0 copy-done
  1.4 0.0 copy-done.1
  1.4 0.6 copy-done.2
  2.0 0.0 copy-done.3
  2.0 0.0 copy-done.4
  2.1 83.8 %cycle.1 = f32[2,32,2048]{2,1,0:T(8,128)S(1)} custom-call(f32[2,32,2048]{2,1,0:T(8,128)S(1)} %bitcast.8, f32[2,2048]{1,0:T(2,128)S(1)} %copy-done, s32[1,128]{1,0:T(1,128)S(1)} %bitcast.9, f32[1,128]{1,0:T(1,128)S(1)} %bitcast.10, f32[1,128]{1,0:T(1,128)S(1)} %bitcast.11, f32[32,128]{1,0:T(8,128)S(1)} %copy-done.1), custom_call_target="tpu_custom_call" | custom-call | tf_op jit(solution)/shard_map/cycle/pallas_call | solution.py:551
  85.9 1.2 %copy.8 = f32[32,2,2048]{2,1,0:T(2,128)} copy(f32[32,2,2048]{2,0,1:T(8,128)S(1)} %bitcast.7) | data formatting | bytes 1048576 | tf_op jit(solution)/shard_map/transpose | solution.py:584
Async XLA Ops:
  0.0 1.4 %copy-start = (f32[2,2048]{1,0:T(2,128)S(1)}, f32[2,2048]{1,0:T(2,128)}, u32[]{:S(2)}) copy-start(f32[2,2048]{1,0:T(2,128)} %args_1_.4) | copy-start | bytes 49156
  0.0 1.4 %copy-start.1 = (f32[32,128]{1,0:T(8,128)S(1)}, f32[32,128]{1,0:T(8,128)}, u32[]{:S(2)}) copy-start(f32[32,128]{1,0:T(8,128)} %args_5_.4) | copy-start | bytes 49156
  1.4 0.7 copy-start.2
  1.4 0.7 copy-start.3
  1.4 0.7 copy-start.4

commit v8 on v7

--- a/solution.py
+++ b/solution.py
@@ -179,14 +179,11 @@
     observed = observed[:mdev] + observed[mdev:2 * mdev] + observed[2 * mdev:]
     ab[REACH, mine, :] = observed
 
-    def send_obs(i, c):
+    for i in (4, 3, 5, 2, 6, 1, 7):
         pltpu.make_async_remote_copy(
             src_ref=ab.at[REACH, mine], dst_ref=ab.at[REACH, mine],
             send_sem=ssem.at[S_OBS], recv_sem=rsem.at[R_OBS + i],
             device_id={"mem": other(me_m, i, mem_count)}, device_id_type=MESH).start()
-        return c
-
-    lax.fori_loop(1, mem_count, send_obs, 0)
 
     right = other(me_m, 1, mem_count)
     left = other(me_m, mem_count - 1, mem_count)

time: 87.2 us -> 87.9 us (level)
  no operation moved by 1% of the time
where the time goes in v8:
time: 87.9 us; the launch traced here: 87.8 us
  Pallas kernels  84.5 us (96%)
  local copies, waits for them, and re-layouts  3.22 us (4%)
    pallas_call x1, Pallas kernels, shards(): pl.pallas_call(call, out_shape=jax.ShapeDtypeStruct((pdev, mdev, slab), f...  84.5 us
    unnamed x11, local copies, waits for them, and re-layouts  2.02 us

profile of v8, /device:TPU:1, one launch (start us, length us, event | category | flops | bytes accessed | tf_op | source)
XLA Modules:
  0.0 87.8 jit_solution(13357406203457200373)
XLA Ops:
  0.0 0.0 copy-start
  0.0 0.0 copy-start.1
  0.0 1.4 %copy.10 = f32[32,2,2048]{2,0,1:T(8,128)S(1)} copy(f32[32,2,2048]{2,1,0:T(2,128)} %param.6) | data formatting | bytes 1048576 | tf_op args[0]
  1.4 0.0 copy-start.2
  1.4 0.0 copy-start.3
  1.4 0.0 copy-start.4
  1.4 0.0 copy-done
  1.4 0.0 copy-done.1
  1.4 0.6 copy-done.2
  2.0 0.0 copy-done.3
  2.0 0.0 copy-done.4
  2.1 84.5 %cycle.1 = f32[2,32,2048]{2,1,0:T(8,128)S(1)} custom-call(f32[2,32,2048]{2,1,0:T(8,128)S(1)} %bitcast.8, f32[2,2048]{1,0:T(2,128)S(1)} %copy-done, s32[1,128]{1,0:T(1,128)S(1)} %bitcast.9, f32[1,128]{1,0:T(1,128)S(1)} %bitcast.10, f32[1,128]{1,0:T(1,128)S(1)} %bitcast.11, f32[32,128]{1,0:T(8,128)S(1)} %copy-done.1), custom_call_target="tpu_custom_call" | custom-call | tf_op jit(solution)/shard_map/cycle/pallas_call | solution.py:548
  86.6 1.2 %copy.8 = f32[32,2,2048]{2,1,0:T(2,128)} copy(f32[32,2,2048]{2,0,1:T(8,128)S(1)} %bitcast.7) | data formatting | bytes 1048576 | tf_op jit(solution)/shard_map/transpose | solution.py:581
Async XLA Ops:
  0.0 1.4 %copy-start = (f32[2,2048]{1,0:T(2,128)S(1)}, f32[2,2048]{1,0:T(2,128)}, u32[]{:S(2)}) copy-start(f32[2,2048]{1,0:T(2,128)} %args_1_.4) | copy-start | bytes 49156
  0.0 1.4 %copy-start.1 = (f32[32,128]{1,0:T(8,128)S(1)}, f32[32,128]{1,0:T(8,128)}, u32[]{:S(2)}) copy-start(f32[32,128]{1,0:T(8,128)} %args_5_.4) | copy-start | bytes 49156
  1.4 0.7 copy-start.2
  1.4 0.7 copy-start.3
  1.4 0.7 copy-start.4
